TPU v7x, 256 devices: a whole 4x4x8 slice. The times are simulated.
256 devices in a mesh: mode: 64 (over y, z, core), row: 4 (over x).
Axes of the slice: x: 4, y: 4, z: 8, core: 2. Of those that a mesh axis runs over, the one named last changes fastest.
Arguments:
- density: float32 [2, 2048, 2048], P(None, 'row', 'mode'), may hold values from -6 to 6
- auxiliary: float32 [2048, 256, 2, 128], P('row', 'mode'), may hold values from -2 to 2
- hamiltonian: bfloat16 [2048, 2048], P('row'), as said below
- coupling: int32 [2, 128], replicated, may hold values from 0 to 2047, as said below
- lead_index: int32 [256], P('mode'), may hold values from 0 to 1
- mode_level: float32 [256], P('mode'), may hold values from -2 to 2
- mode_width: float32 [256], P('mode'), may hold values from 0.05 to 3
- residue: float32 [256, 2], P('mode'), may hold values from -4 to 4
- occupation: float32 [256], P('mode'), may hold values from 0 to 1
- lead_gamma: bfloat16 [2, 128, 128], replicated, may hold values from -0.5 to 0.5
Outputs:
- density_rate: float32 [2, 2048, 2048], P(None, 'row', 'mode')
- auxiliary_rate: float32 [2048, 256, 2, 128], P('row', 'mode')
Inputs may be any that keep to these rules, and one draw needn't show every extreme that they name: `coupling`: all 256 entries are distinct orbitals. `hamiltonian`: Symmetric.
All inputs are finite; a program needn't handle non-finite values.
Results may differ from a plain program's by a relative error of at most 0.0044.
Values may be sent and summed in bfloat16 or wider, within the bound.
A program may use at most 128 MiB of HBM per device.

v0:
```python
import jax
import jax.numpy as jnp
from jax import lax
from jax.sharding import PartitionSpec as P

H2 = 0.05
F32 = jnp.float32
BF = jnp.bfloat16


def dot(a, b, ca=1, cb=0):
    return lax.dot_general(a, b, (((ca,), (cb,)), ((), ())), preferred_element_type=F32)


def over_row(x):
    devices = lax.axis_size("row")
    return lax.all_to_all(jnp.broadcast_to(x[None], (devices, *x.shape)), "row", 0, 0, tiled=True)


def by_lead(x, gamma):
    leads, coupled = gamma.shape[:2]
    return jnp.concatenate(
        [dot(x[:, l * coupled : (l + 1) * coupled], gamma[l]) for l in range(leads)], axis=1
    )


def shards(density, auxiliary, hamiltonian, coupling, lead_index, mode_level, mode_width, residue, occupation, lead_gamma):
    rows, cols = density.shape[1:]
    n = hamiltonian.shape[1]
    leads, coupled = coupling.shape
    q = leads * coupled
    modes = auxiliary.shape[1]
    n_mode = lax.axis_size("mode")
    n_row = lax.axis_size("row")
    x_pos, m_pos = lax.axis_index("row"), lax.axis_index("mode")
    row_start, col_start = x_pos * rows, m_pos * cols
    flat = coupling.reshape(-1)

    e_full = (jnp.arange(n, dtype=jnp.int32)[:, None] == flat[None, :]).astype(BF)
    e_row = (row_start + jnp.arange(rows, dtype=jnp.int32)[:, None] == flat[None, :]).astype(BF)
    e_col = (col_start + jnp.arange(cols, dtype=jnp.int32)[:, None] == flat[None, :]).astype(BF)
    g_row = by_lead(e_row, lead_gamma).astype(BF)
    g_col = by_lead(e_col, lead_gamma).astype(BF)

    rho_t = jnp.swapaxes(density, 1, 2).astype(BF).reshape(2 * cols, rows)
    ham_ct = jnp.swapaxes(lax.dynamic_slice_in_dim(hamiltonian, col_start, cols, 1), 0, 1)

    first = over_row(jnp.concatenate([ham_ct, rho_t], axis=0))
    first = jnp.moveaxis(first, 0, 1).reshape(3 * cols, n)
    ham_c = first[:cols]
    applied = dot(first, hamiltonian, 1, 1)
    ham2_ct = applied[:cols].astype(BF)
    hrho_t = applied[cols:]
    he_row = dot(hamiltonian, e_full)
    hg_row = by_lead(he_row.astype(BF), lead_gamma)
    he_col = dot(ham_c, e_full).astype(BF)
    hg_col = by_lead(he_col, lead_gamma)

    panel = lax.all_gather(rho_t.reshape(2, cols, rows), "mode", axis=1, tiled=True)
    ham2_all = lax.all_gather(ham2_ct, "mode", axis=0, tiled=True)
    pi_b = auxiliary.astype(BF).reshape(rows, modes * 2 * coupled)
    pi_all = lax.all_gather(pi_b, "row", axis=0, tiled=True)

    onehot = (lead_index[:, None] == jnp.arange(leads, dtype=jnp.int32)[None, :]).astype(F32)
    lam_re, lam_im = -mode_width, mode_level
    l_parts, m_parts = [[], []], [[], []]
    for l in range(leads):
        s = [sum(onehot[k, l] * auxiliary[:, k, p] for k in range(modes)) for p in range(2)]
        m_re = sum(onehot[k, l] * (lam_re[k] * auxiliary[:, k, 0] - lam_im[k] * auxiliary[:, k, 1]) for k in range(modes))
        m_im = sum(onehot[k, l] * (lam_re[k] * auxiliary[:, k, 1] + lam_im[k] * auxiliary[:, k, 0]) for k in range(modes))
        for p in range(2):
            l_parts[p].append(s[p])
        m_parts[0].append(m_re)
        m_parts[1].append(m_im)
    l_part = jnp.concatenate(l_parts[0] + l_parts[1], axis=1)
    m_part = jnp.concatenate(m_parts[0] + m_parts[1], axis=1)
    w_l = jnp.concatenate([(residue[:, p][:, None] * onehot).sum(0) for p in range(2)])
    v_l = jnp.concatenate([((residue[:, p] * occupation)[:, None] * onehot).sum(0) for p in range(2)])

    hrho_b = hrho_t.astype(BF)
    f_re = dot(jnp.concatenate([hrho_b[cols:], rho_t[cols:]], 0), jnp.concatenate([2 * g_col, -hg_col.astype(BF)], 0), 0, 0)
    f_im = dot(jnp.concatenate([hrho_b[:cols], rho_t[:cols]], 0), jnp.concatenate([-2 * g_col, hg_col.astype(BF)], 0), 0, 0)
    f_part = jnp.concatenate([f_re, f_im], axis=1)
    l_part_b = l_part.astype(BF)
    n_part = jnp.concatenate([dot(l_part_b[:, :q], g_row, 0, 0), -dot(l_part_b[:, q:], g_row, 0, 0)], axis=1)

    piece = rows // n_mode
    n_piece = q // n_mode
    scal = jnp.concatenate([w_l, v_l])
    scal = jnp.zeros((n_mode, 1, 2 * q), F32).at[:, 0, : scal.shape[0]].set(scal)
    payload = jnp.concatenate(
        [a.reshape(n_mode, -1, 2 * q) for a in (l_part, m_part, f_part, n_part)] + [scal], axis=1
    )
    mine = lax.psum_scatter(payload, "mode", scatter_dimension=0, tiled=True)[0]
    n_mine = over_row(mine[3 * piece : 3 * piece + n_piece]).sum(0)
    w_sum, v_sum = mine[-1, : 2 * leads], mine[-1, 2 * leads : 4 * leads]
    mine = jnp.concatenate([mine[: 3 * piece], n_mine], axis=0).astype(BF)
    whole = lax.all_gather(mine, "mode", axis=0, tiled=False)
    l1_b = whole[:, :piece].reshape(rows, 2 * q)
    m1 = whole[:, piece : 2 * piece].reshape(rows, 2 * q).astype(F32)
    f_all = whole[:, 2 * piece : 3 * piece].reshape(rows, 2 * q).astype(F32)
    n_all = whole[:, 3 * piece :].reshape(q, 2 * q)

    grow_full = by_lead(e_full, lead_gamma).astype(BF)
    src = jnp.concatenate([dot(panel[p], grow_full, 0, 0) for p in range(2)], axis=1)
    w_q = jnp.repeat(w_sum, coupled)
    v_q = jnp.repeat(v_sum, coupled)
    s_re, s_im = src[:, :q], src[:, q:]
    g_row_f = g_row.astype(F32)
    drive = jnp.concatenate(
        [w_q[:q] * s_re - w_q[q:] * s_im - (v_q[:q] - v_q[q:]) * g_row_f, w_q[:q] * s_im + w_q[q:] * s_re - (v_q[:q] + v_q[q:]) * g_row_f], axis=1
    )
    x_row = (3.0 * l1_b.astype(F32) + 2 * H2 * (m1 + drive)).astype(BF)
    p1 = jnp.concatenate([dot(e_col, l1_b[:, p * q : (p + 1) * q], 1, 1) for p in range(2)], 0)
    xe = jnp.concatenate([dot(e_col, x_row[:, p * q : (p + 1) * q], 1, 1) for p in range(2)], 0)
    rhoh_t = jnp.concatenate([dot(ham_c, panel[p]) for p in range(2)], 0)
    y = hrho_t - 2.0 * rhoh_t + 2.0 * jnp.concatenate([-p1[cols:], p1[:cols]], 0)
    z = dot(lax.dynamic_slice_in_dim(ham_c, row_start, rows, 1), l1_b)
    owner = col_start // rows
    own_l = lax.dynamic_slice_in_dim(l1_b, col_start - owner * rows, cols, 0)
    own_x = lax.dynamic_slice_in_dim(x_row, col_start - owner * rows, cols, 0)
    mask = (x_pos == owner).astype(BF)
    second = over_row(jnp.concatenate([y.astype(BF), ham2_ct], 0))
    second = jnp.moveaxis(second, 0, 1).reshape(3 * cols, n)
    third = over_row(jnp.concatenate([z.astype(BF), own_l * mask, own_x * mask], 0)).astype(F32).sum(0)
    z, l_c, x_c = third[:cols], third[cols : 2 * cols], third[2 * cols :]
    hy = dot(second[: 2 * cols], hamiltonian, 1, 1)
    ham2_c = second[2 * cols :]
    rhoh2_t = jnp.concatenate([dot(ham2_c, panel[p]) for p in range(2)], 0)
    b_re = x_c[:, :q] + 4 * H2 * z[:, q:]
    b_im = -x_c[:, q:] + 4 * H2 * z[:, :q]
    back_re = dot(b_re.astype(BF), e_row, 1, 1)
    back_im = dot(b_im.astype(BF), e_row, 1, 1)
    l_cb = l_c.astype(BF)
    he_row_b = he_row.astype(BF)
    c1_re, c1_im = dot(l_cb[:, :q], he_row_b, 1, 1), -dot(l_cb[:, q:], he_row_b, 1, 1)
    c2_re, c2_im = dot(he_col, l1_b[:, :q], 1, 1), dot(he_col, l1_b[:, q:], 1, 1)
    d_re, d_im = c1_re - c2_re, c1_im - c2_im
    comm = hrho_t - rhoh_t
    base = -2 * H2 * (hy + rhoh2_t) + xe
    out_re = 3.0 * comm[cols:] + base[:cols] + back_re + 2 * H2 * d_im
    out_im = -3.0 * comm[:cols] + base[cols:] + back_im - 2 * H2 * d_re
    density_rate = jnp.swapaxes(jnp.stack([out_re, out_im]), 1, 2)

    h_pi = dot(hamiltonian, pi_all).reshape(rows, modes, 2, coupled)
    h2_pi = dot(ham2_all, pi_all.reshape(n, -1), 0, 0).reshape(rows, modes, 2, coupled)
    lg = jnp.concatenate([by_lead(l1_b[:, p * q : (p + 1) * q], lead_gamma) for p in range(2)], 1)
    u = 2 * H2 * (f_all + lg + dot(e_row, n_all))
    outs = []
    for k in range(modes):
        is0 = onehot[k, 0] > 0

        def pick(a):
            return jnp.where(is0, a[:, :coupled], a[:, coupled:])

        lr, li = lam_re[k], lam_im[k]
        wr, wi, occ = residue[k, 0], residue[k, 1], occupation[k]
        sr, si, ur, ui = pick(s_re), pick(s_im), pick(u[:, :q]), pick(u[:, q:])
        gk, hgk = pick(g_row_f), pick(hg_row)
        br, bi = sr - occ * gk, si - occ * gk
        ar, ai = 3 + 2 * H2 * lr, 2 * H2 * li
        tr = ar * br - ai * bi + ur - 2 * H2 * occ * hgk
        ti = ar * bi + ai * br + ui + 2 * H2 * occ * hgk
        pr, pim = auxiliary[:, k, 0], auxiliary[:, k, 1]
        cr = 3 * lr + 2 * H2 * (lr * lr - li * li)
        ci = 3 * li + 4 * H2 * lr * li
        er, ei = 4 * H2 * li, -3 - 4 * H2 * lr
        hr, hi = h_pi[:, k, 0], h_pi[:, k, 1]
        outs.append(cr * pr - ci * pim + er * hr - ei * hi - 2 * H2 * h2_pi[:, k, 0] + wr * tr - wi * ti)
        outs.append(cr * pim + ci * pr + er * hi + ei * hr - 2 * H2 * h2_pi[:, k, 1] + wr * ti + wi * tr)
    auxiliary_rate = jnp.stack(outs, axis=1).reshape(rows, modes, 2, coupled)
    return density_rate, auxiliary_rate


def solution(mesh):
    in_specs = (
        P(None, "row", "mode"),
        P("row", "mode", None, None),
        P("row", None),
        P(),
        P("mode"),
        P("mode"),
        P("mode"),
        P("mode", None),
        P("mode"),
        P(),
    )
    out_specs = (P(None, "row", "mode"), P("row", "mode", None, None))
    return jax.shard_map(shards, mesh=mesh, in_specs=in_specs, out_specs=out_specs, check_vma=False)
```

profile of v0, /device:TPU:1, one launch (start us, length us, event | category | flops | bytes accessed | tf_op | source)
XLA Modules:
  0.0 596.0 jit_solution(17959333989548009049)
XLA Ops:
  9.8 4.8 all-to-all-start
  14.7 4.1 fusion.164
  21.0 6.2 %convert_bitcast_fusion.1 = (bf16[512,128]{1,0:T(8,128)(2,1)}, f32[512,1,1,128]{3,0,2,1:T(8,128)}, bf16[512,128]{1,0:T(8,128)(2,1)}, f32[512,1,1,128]{3,0,2,1:T(...) fusion(f32[512,1,1,128]{3,0,2,1:T(8,128)S(1)} %bitcast.292, ...), kind=kLoop, calls=%fused_computation.175 | loop fusion | flops 2097152 | bytes 3670048 | tf_op jit(solution)/shard_map/add | solution.py:68
  27.2 8.4 %add_bitcast_fusion = f32[64,8,128]{2,1,0:T(8,128)} fusion(f32[]{:T(128)} %bitcast.15, f32[]{:T(128)} %bitcast.14, f32[]{:T(128)} %bitcast.13, f32[]{:T(128)} %bitcast.12, f32[512,1,1,128]{3,0,2,1:T(8,128)S(1)} %bitcast.272, f32[]{:T(128)} %bitcast.20, f32[512,1,1,128]{3,0,2,1:T(8,128)S(1)} %bitcast.279, f32[]{:T(128)} %bitcast.19, ...), kind=kLoop, calls=%fused_computation.101 | loop fusion | flops 1245184 | bytes 2359344 | tf_op jit(solution)/shard_map/add | solution.py:70
  35.6 8.4 %add_bitcast_fusion.1 = f32[64,8,128]{2,1,0:T(8,128)} fusion(f32[]{:T(128)} %bitcast.10, f32[]{:T(128)} %bitcast.9, f32[]{:T(128)} %bitcast.8, f32[]{:T(128)} %bitcast.7, f32[512,1,1,128]{3,0,2,1:T(8,128)S(1)} %bitcast.273, f32[]{:T(128)} %bitcast.20, f32[512,1,1,128]{3,0,2,1:T(8,128)S(1)} %bitcast.280, f32[]{:T(128)} %bitcast.19, ...), kind=kLoop, calls=%fused_computation.102 | loop fusion | flops 1245184 | bytes 2359344 | tf_op jit(solution)/shard_map/add | solution.py:70
  44.1 8.5 %add_bitcast_fusion.2 = f32[64,8,128]{2,1,0:T(8,128)} fusion(f32[]{:T(128)} %bitcast.15, f32[]{:T(128)} %bitcast.14, f32[]{:T(128)} %bitcast.13, f32[]{:T(128)} %bitcast.12, f32[512,1,1,128]{3,0,2,1:T(8,128)S(1)} %bitcast.281, f32[]{:T(128)} %bitcast.20, f32[512,1,1,128]{3,0,2,1:T(8,128)S(1)} %bitcast.274, f32[]{:T(128)} %bitcast.19, ...), kind=kLoop, calls=%fused_computation.103 | loop fusion | flops 1245184 | bytes 2359344 | tf_op jit(solution)/shard_map/add | solution.py:69
  52.6 8.4 %add_bitcast_fusion.3 = f32[64,8,128]{2,1,0:T(8,128)} fusion(f32[]{:T(128)} %bitcast.10, f32[]{:T(128)} %bitcast.9, f32[]{:T(128)} %bitcast.8, f32[]{:T(128)} %bitcast.7, f32[512,1,1,128]{3,0,2,1:T(8,128)S(1)} %bitcast.282, f32[]{:T(128)} %bitcast.20, f32[512,1,1,128]{3,0,2,1:T(8,128)S(1)} %bitcast.275, f32[]{:T(128)} %bitcast.19, ...), kind=kLoop, calls=%fused_computation.104 | loop fusion | flops 1245184 | bytes 2359344 | tf_op jit(solution)/shard_map/add | solution.py:69
  67.0 2.1 copy.205
  69.0 2.0 reshape.500
  71.1 2.3 pad_maximum_fusion
  80.8 2.5 copy.202
  84.1 13.7 %concatenate.113 = f32[64,29,512]{2,1,0:T(8,128)} concatenate(f32[64,8,512]{2,1,0:T(8,128)} %pad_maximum_fusion, f32[64,8,512]{2,1,0:T(8,128)} %pad_maximum_fusion.1, f32[64,8,512]{2,1,0:T(8,128)} %bitcast.327, f32[64,4,512]{2,1,0:T(4,128)} %reshape.500, f32[64,1,512]{2,1,0:T(1,128)} %scatter.8), dimensions={1} | concatenate | bytes 7602176 | tf_op jit(solution)/shard_map/concatenate | solution.py:91
  99.4 3.3 convert_element_type.100
  102.6 2.6 reshape.502
  144.5 96.6 %reduce-scatter.2.cloned.1.call-done = f32[1,29,512]{2,1,0:T(8,128)} async-done(((f32[64,29,512]{2,1,0:T(8,128)}), f32[1,29,512]{2,1,0:T(8,128)}) %reduce-scatter.2.cloned.1.call-update) | async-done | bytes 59408 | tf_op jit(solution)/shard_map/reduce_scatter | solution.py:94
  242.4 3.8 all-to-all-start.1
  251.2 74.0 %all-gather.11.cloned.1.call-done = bf16[2048,512]{1,0:T(8,128)(2,1)} async-done(((bf16[32,512]{1,0:T(8,128)(2,1)}), bf16[2048,512]{1,0:T(8,128)(2,1)}) %all-gather.11.cloned.1.call-update) | async-done | bytes 2097168 | tf_op jit(solution)/shard_map/all_gather | solution.py:60
  325.2 49.4 %all-gather.9.cloned.1.call-done = bf16[2048,1024]{1,0:T(8,128)(2,1)} async-done(((bf16[512,1024]{1,0:T(8,128)(2,1)}), bf16[2048,1024]{1,0:T(8,128)(2,1)}) %all-gather.9.cloned.1.call-update) | async-done | bytes 4194320 | tf_op jit(solution)/shard_map/all_gather | solution.py:62
  374.6 5.2 fusion.173
  383.0 4.6 fusion.172
  415.8 41.6 %all-gather.5.cloned.1.call-done = bf16[2,2048,512]{2,1,0:T(8,128)(2,1)} async-done(((bf16[2,32,512]{2,1,0:T(8,128)(2,1)}), bf16[2,2048,512]{2,1,0:T(8,128)(2,1)}) %all-gather.5.cloned.1.call-update) | async-done | bytes 4194320 | tf_op jit(solution)/shard_map/all_gather | solution.py:59
  457.5 3.0 fusion.8
  460.5 2.8 select_subtract_fusion.1
  463.3 2.0 multiply_subtract_fusion.1
  465.3 2.8 select_subtract_fusion
  471.8 62.8 %all-gather.7.cloned.1.call-done = bf16[64,28,512]{2,1,0:T(8,128)(2,1)} async-done(((bf16[1,28,512]{2,1,0:T(8,128)(2,1)}), bf16[64,28,512]{2,1,0:T(8,128)(2,1)}) %all-gather.7.cloned.1.call-update) | async-done | bytes 1835024 | tf_op jit(solution)/shard_map/all_gather | solution.py:98
  544.3 4.3 all-to-all-start.2
  552.2 1.9 fusion.6
  566.6 2.9 copy.232
  572.5 4.0 all-to-all-start.3
  579.1 4.3 all-to-all-done.3
  584.5 2.4 fusion.4
  (322 shorter events, 104.8 us)
Async XLA Ops:
  7.2 7.5 %copy-start.51 = (f32[2,512,32]{1,2,0:T(8,128)S(1)}, f32[2,512,32]{1,2,0:T(8,128)}, u32[]{:S(2)}) copy-start(f32[2,512,32]{1,2,0:T(8,128)} %param.12) | copy-start | bytes 393220
  9.8 65.5 %all-to-all-start = ((bf16[4,96,512]{2,1,0:T(8,128)(2,1)}), bf16[4,96,512]{2,1,0:T(8,128)(2,1)}, u32[]{:S(2)}, u32[]{:S(2)}) async-start(bf16[4,96,512]{2,1,0:T(8,128)(2,1)} %broadcast_in_dim.18), calls=%async_computation | async-start | bytes 786432 | tf_op jit(solution)/shard_map/all_to_all | solution.py:17
  14.6 226.4 %reduce-scatter.2.cloned.1.call-start = ((), (), s32[]{:S(2)}) async-start(), calls=%async_computation.6 | async-start | bytes 4259840 | tf_op jit(solution)/shard_map/reduce_scatter | solution.py:94
  14.7 60.0 %copy-start.48 = (bf16[2,32,512]{2,1,0:T(8,128)(2,1)}, bf16[2,32,512]{2,1,0:T(8,128)(2,1)S(1)}, u32[]{:S(2)}) copy-start(bf16[2,32,512]{2,1,0:T(8,128)(2,1)S(1)} %convert_bitcast_fusion.5) | copy-start | bytes 196612
  18.8 33.8 %copy-start.1 = (f32[512,1,1,128]{3,2,1,0:T(1,128)}, f32[512,1,1,128]{3,2,1,0:T(1,128)S(1)}, u32[]{:S(2)}) copy-start(f32[512,1,1,128]{3,2,1,0:T(1,128)S(1)} %get-tuple-element.71) | copy-start | bytes 786436
  18.8 33.8 %copy-start.3 = (f32[512,1,1,128]{3,2,1,0:T(1,128)}, f32[512,1,1,128]{3,2,1,0:T(1,128)S(1)}, u32[]{:S(2)}) copy-start(f32[512,1,1,128]{3,2,1,0:T(1,128)S(1)} %get-tuple-element.68) | copy-start | bytes 786436
  18.8 33.7 %copy-start.5 = (f32[512,1,1,128]{3,2,1,0:T(1,128)}, f32[512,1,1,128]{3,2,1,0:T(1,128)S(1)}, u32[]{:S(2)}) copy-start(f32[512,1,1,128]{3,2,1,0:T(1,128)S(1)} %get-tuple-element.72) | copy-start | bytes 786436
  44.1 17.4 %copy-start.65 = (s32[2,128]{1,0:T(2,128)S(1)}, s32[2,128]{1,0:T(2,128)}, u32[]{:S(2)}) copy-start(s32[2,128]{1,0:T(2,128)} %param.15) | copy-start | bytes 3076
  44.1 17.5 %copy-start.24 = (bf16[2,128,128]{2,1,0:T(8,128)(2,1)S(1)}, bf16[2,128,128]{2,1,0:T(8,128)(2,1)}, u32[]{:S(2)}) copy-start(bf16[2,128,128]{2,1,0:T(8,128)(2,1)} %param.21) | copy-start | bytes 196612
  64.9 6.2 %copy-start.71 = (f32[4,2]{0,1:T(2,128)S(1)}, f32[4,2]{0,1:T(2,128)}, u32[]{:S(2)}) copy-start(f32[4,2]{0,1:T(2,128)} %param.19) | copy-start | bytes 100
  64.9 6.2 %copy-start.80 = (f32[4]{0:T(128)S(1)}, f32[4]{0:T(128)}, u32[]{:S(2)}) copy-start(f32[4]{0:T(128)} %param.20) | copy-start | bytes 52
  97.8 227.4 %all-gather.11.cloned.1.call-start = ((), (), s32[]{:S(2)}) async-start(), calls=%async_computation.9 | async-start | bytes 2129920 | tf_op jit(solution)/shard_map/all_gather | solution.py:60
  99.3 275.3 %all-gather.9.cloned.1.call-start = ((), (), s32[]{:S(2)}) async-start(), calls=%async_computation.8 | async-start | bytes 5242880 | tf_op jit(solution)/shard_map/all_gather | solution.py:62
  105.2 352.2 %all-gather.5.cloned.1.call-start = ((), (), s32[]{:S(2)}) async-start(), calls=%async_computation.5 | async-start | bytes 4259840 | tf_op jit(solution)/shard_map/all_gather | solution.py:59
  242.4 8.1 %all-to-all-start.1 = ((f32[4,4,512]{2,1,0:T(4,128)}), f32[4,4,512]{2,1,0:T(4,128)S(1)}, u32[]{:S(2)}, u32[]{:S(2)}) async-start(f32[4,4,512]{2,1,0:T(4,128)} %broadcast_in_dim.20), calls=%async_computation.2 | async-start | bytes 65536 | tf_op jit(solution)/shard_map/all_to_all | solution.py:17
  246.2 288.4 %all-gather.7.cloned.1.call-start = ((), (), s32[]{:S(2)}) async-start(), calls=%async_computation.7 | async-start | bytes 2129920 | tf_op jit(solution)/shard_map/all_gather | solution.py:98
  415.8 47.4 %copy-start.86 = (f32[256]{0:T(256)S(1)}, f32[256]{0:T(256)}, u32[]{:S(2)}) copy-start(f32[256]{0:T(256)} %broadcast_bitcast_fusion.1) | copy-start | bytes 3076
  415.8 47.4 %copy-start.87 = (f32[256]{0:T(256)S(1)}, f32[256]{0:T(256)}, u32[]{:S(2)}) copy-start(f32[256]{0:T(256)} %broadcast_bitcast_fusion.2) | copy-start | bytes 3076
  415.8 47.4 %copy-start.88 = (f32[256]{0:T(256)S(1)}, f32[256]{0:T(256)}, u32[]{:S(2)}) copy-start(f32[256]{0:T(256)} %broadcast_bitcast_fusion.3) | copy-start | bytes 3076
  415.8 47.4 %copy-start.89 = (f32[256]{0:T(256)S(1)}, f32[256]{0:T(256)}, u32[]{:S(2)}) copy-start(f32[256]{0:T(256)} %broadcast_bitcast_fusion) | copy-start | bytes 3076
  470.7 65.1 %copy-start.78 = (s32[32]{0:T(128)S(1)}, s32[32]{0:T(128)}, u32[]{:S(2)}) copy-start(s32[32]{0:T(128)} %copy-done.77) | copy-start | bytes 388
  471.8 66.7 %copy-start.66 = (s32[2,128]{1,0:T(2,128)S(1)}, s32[2,128]{1,0:T(2,128)}, u32[]{:S(2)}) copy-start(s32[2,128]{1,0:T(2,128)} %param.15) | copy-start | bytes 3076
  535.8 6.1 %copy-start.7 = (bf16[512,512]{1,0:T(8,128)(2,1)}, bf16[512,512]{1,0:T(8,128)(2,1)S(1)}, u32[]{:S(2)}) copy-start(bf16[512,512]{1,0:T(8,128)(2,1)S(1)} %slice_bitcast_fusion.14) | copy-start | bytes 1572868
  536.2 6.6 %copy-start.47 = (f32[96,512]{1,0:T(8,128)S(1)}, f32[96,512]{1,0:T(8,128)}, u32[]{:S(2)}) copy-start(f32[96,512]{1,0:T(8,128)} %copy-done.46) | copy-start | bytes 589828
  536.2 6.6 %copy-start.69 = (f32[32,512]{1,0:T(8,128)S(1)}, f32[32,512]{1,0:T(8,128)}, u32[]{:S(2)}) copy-start(f32[32,512]{1,0:T(8,128)} %fusion.5) | copy-start | bytes 196612
  536.3 6.6 %copy-start.70 = (f32[32,512]{1,0:T(8,128)S(1)}, f32[32,512]{1,0:T(8,128)}, u32[]{:S(2)}) copy-start(f32[32,512]{1,0:T(8,128)} %fusion.2) | copy-start | bytes 196612
  536.3 7.2 %copy-start.53 = (bf16[32,512]{1,0:T(8,128)(2,1)S(1)}, bf16[32,512]{1,0:T(8,128)(2,1)}, u32[]{:S(2)}) copy-start(bf16[32,512]{1,0:T(8,128)(2,1)} %slice.1048) | copy-start | bytes 98308
  540.2 12.0 %copy-start.73 = (s32[512]{0:T(512)S(1)}, s32[512]{0:T(512)}, u32[]{:S(2)}) copy-start(s32[512]{0:T(512)} %copy-done.72) | copy-start | bytes 6148
  544.3 27.4 %all-to-all-start.2 = ((bf16[4,96,512]{2,1,0:T(8,128)(2,1)}), bf16[4,96,512]{2,1,0:T(8,128)(2,1)}, u32[]{:S(2)}, u32[]{:S(2)}) async-start(bf16[4,96,512]{2,1,0:T(8,128)(2,1)} %broadcast_in_dim.21), calls=%async_computation.3 | async-start | bytes 786432 | tf_op jit(solution)/shard_map/all_to_all | solution.py:17
  569.5 13.9 %copy-start.15 = (bf16[256,512]{1,0:T(8,128)(2,1)S(1)}, bf16[256,512]{1,0:T(8,128)(2,1)}, u32[]{:S(2)}) copy-start(bf16[256,512]{1,0:T(8,128)(2,1)} %copy-done.13) | copy-start | bytes 786436
  570.9 12.9 %copy-start.8 = (bf16[512,512]{1,0:T(8,128)(2,1)S(1)}, bf16[512,512]{1,0:T(8,128)(2,1)}, u32[]{:S(2)}) copy-start(bf16[512,512]{1,0:T(8,128)(2,1)} %copy-done.7) | copy-start | bytes 1572868
  572.5 10.8 %all-to-all-start.3 = ((bf16[4,96,512]{2,1,0:T(8,128)(2,1)}), bf16[4,96,512]{2,1,0:T(8,128)(2,1)S(1)}, u32[]{:S(2)}, u32[]{:S(2)}) async-start(bf16[4,96,512]{2,1,0:T(8,128)(2,1)} %broadcast_in_dim.26), calls=%async_computation.4 | async-start | bytes 786432 | tf_op jit(solution)/shard_map/all_to_all | solution.py:17
  (69 other events, 178.4 us)
Sparse Core Ops, SparseCore 0:
  97.9 143.1 reduce-scatter.1
  243.9 81.2 all-gather.10
  327.0 47.5 all-gather.8
  377.3 80.1 all-gather.4
  460.1 74.4 all-gather.6
where the time goes:
time: 599 us; the launch traced here: 596 us
  waiting for transfers between devices  329 us (55%)
  local copies, waits for them, and re-layouts  86.9 us (15%)
  other arithmetic  74.6 us (12%)
  between operations  45.6 us (8%)
  matrix products  42.4 us (7%)
  starting transfers between devices  17.1 us (3%)
    reduce_scatter x1, waiting for transfers between devices, shards(): mine = lax.psum_scatter(payload, 'mode', scatter_dimension=0, tiled=True)[0]  96.6 us
    all_gather x1, waiting for transfers between devices, shards(): ham2_all = lax.all_gather(ham2_ct, 'mode', axis=0, tiled=True)  74 us
    all_gather x1, waiting for transfers between devices, shards(): whole = lax.all_gather(mine, 'mode', axis=0, tiled=False)  62.8 us
    all_gather x1, waiting for transfers between devices, shards(): pi_all = lax.all_gather(pi_b, 'row', axis=0, tiled=True)  49.4 us
    dot_general x42, matrix products, dot(): lax.dot_general(a, b, (((ca,), (cb,)), ((), ())), preferred_element_type=...  42.4 us
    all_gather x1, waiting for transfers between devices, shards(): lax.all_gather(rho_t.reshape(2, cols, rows), 'mode', axis=1, tiled=True)  41.6 us
    unnamed x204, local copies, waits for them, and re-layouts  38 us
    all_to_all x4, starting transfers between devices, over_row(): lax.all_to_all(jnp.broadcast_to(x[None], (devices, *x.shape)), 'row', 0,...  17 us
  transfers between devices with their start and end apart: 9, of which 6 were waited for; matrix products, arithmetic and copies ran while one was open for 27% of the time, Pallas kernels for 0%

commit v1 on v0

--- a/solution.py
+++ b/solution.py
@@ -1,6 +1,8 @@
 import jax
 import jax.numpy as jnp
 from jax import lax
+from jax.experimental import pallas as pl
+from jax.experimental.pallas import tpu as pltpu
 from jax.sharding import PartitionSpec as P
 
 H2 = 0.05
@@ -12,9 +14,286 @@
     return lax.dot_general(a, b, (((ca,), (cb,)), ((), ())), preferred_element_type=F32)
 
 
-def over_row(x):
-    devices = lax.axis_size("row")
-    return lax.all_to_all(jnp.broadcast_to(x[None], (devices, *x.shape)), "row", 0, 0, tiled=True)
+MESH = pl.DeviceIdType.MESH
+NY, NZ = 4, 8
+
+
+class Net:
+    def __init__(self, send, recv):
+        self.send, self.recv, self.used, self.sent = send, recv, 0, []
+        m = lax.axis_index("mode")
+        self.x = lax.axis_index("row")
+        self.c, self.z, self.y = lax.rem(m, 2), lax.rem(m // 2, NZ), m // (2 * NZ)
+
+    def dev(self, y=None, z=None, c=None, x=None):
+        y = self.y if y is None else y
+        z = self.z if z is None else z
+        c = self.c if c is None else c
+        return {"mode": (y * NZ + z) * 2 + c, "row": self.x if x is None else x}
+
+    def at(self, name, d):
+        size = {"x": 4, "y": NY, "z": NZ}[name]
+        return lax.rem(getattr(self, name) + (d % size), size)
+
+    def slot(self):
+        self.used += 1
+        return self.used - 1
+
+    def start(self, src, dst, to, slot):
+        copy = pltpu.make_async_remote_copy(
+            src_ref=src, dst_ref=dst, send_sem=self.send.at[slot], recv_sem=self.recv.at[slot], device_id=to, device_id_type=MESH
+        )
+        copy.start()
+        self.sent.append(copy)
+
+    def arrive(self, ref, slot):
+        pltpu.make_async_remote_copy(
+            src_ref=ref, dst_ref=ref, send_sem=self.send.at[slot], recv_sem=self.recv.at[slot],
+            device_id=self.dev(c=1 - self.c), device_id_type=MESH,
+        ).wait_recv()
+
+    def finish(self):
+        for copy in self.sent:
+            copy.wait_send()
+
+    def greet(self, peers):
+        barrier = pltpu.get_barrier_semaphore()
+        for peer in peers:
+            pl.semaphore_signal(barrier, inc=1, device_id=peer, device_id_type=MESH)
+        pl.semaphore_wait(barrier, len(peers))
+
+
+def ring(net, name, part, share, t, step):
+    size = {"x": 4, "y": NY, "z": NZ}[name]
+    far = size // 2
+    slots = {(d, s): net.slot() for s in range(1, far + 1) for d in (1, -1)}
+    at = lambda d: net.at(name, d)
+    for d in (1, -1):
+        net.start(part(at(0), None), part(at(0), None), net.dev(**{name: at(d)}), slots[d, 1])
+    share(at(0))
+    for s in range(1, far + 1):
+        yield t + s * step
+        for d in (1, -1):
+            half = None if s < far else (d + 1) // 2
+            net.arrive(part(at(-d * s), half), slots[d, s])
+            if s < far:
+                half = None if s + 1 < far else (d + 1) // 2
+                net.start(part(at(-d * s), half), part(at(-d * s), half), net.dev(**{name: at(d)}), slots[d, s + 1])
+        if s < far:
+            share(at(s))
+            share(at(-s))
+        else:
+            share(at(far))
+
+
+def gather_plane(net, buf, cut, rows, lanes, t, unit):
+    lane = {None: pl.ds(0, lanes), 0: pl.ds(0, lanes // 2), 1: pl.ds(lanes // 2, lanes // 2)}
+    low, high = pl.ds(0, cut), pl.ds(cut, rows - cut)
+    c = net.c
+    waits = []
+
+    def share_of(ref_of):
+        def share(pos):
+            slot = net.slot()
+            mine, theirs = ref_of(pos, c), ref_of(pos, 1 - c)
+            net.start(mine, mine, net.dev(c=1 - c), slot)
+            waits.append((theirs, slot))
+        return share
+
+    def nothing(pos):
+        pass
+
+    def first():
+        yield from ring(net, "y", lambda p, h: buf.at[p, net.z, c, low, lane[h]], nothing, t, 2.0 + unit)
+        yield from ring(
+            net, "z", lambda p, h: buf.at[:, p, c, low, lane[h]],
+            share_of(lambda p, cc: buf.at[:, p, cc, low, lane[None]]), t + 5.0 + 2 * unit, 2.0 + 4 * unit,
+        )
+
+    def second():
+        yield from ring(net, "z", lambda p, h: buf.at[net.y, p, c, high, lane[h]], nothing, t, 2.0 + unit)
+        yield from ring(
+            net, "y", lambda p, h: buf.at[p, :, c, high, lane[h]],
+            share_of(lambda p, cc: buf.at[p, :, cc, high, lane[None]]), t + 9.0 + 4 * unit, 2.0 + 8 * unit,
+        )
+
+    yield from merge([first(), second()])
+    yield t + 12.0 + 30 * unit
+    for ref, slot in waits:
+        net.arrive(ref, slot)
+
+
+def merge(threads):
+    live = []
+    for thread in threads:
+        when = next(thread, None)
+        if when is not None:
+            live.append([when, len(live), thread])
+    while live:
+        live.sort(key=lambda item: (item[0], item[1]))
+        yield live[0][0]
+        when = next(live[0][2], None)
+        if when is None:
+            live.pop(0)
+        else:
+            live[0][0] = when
+
+
+def reduce_plane(net, pay, whole, pair, acc, got1, got2, gotz, xs_out, xs_in, keep_rows):
+    c, y, z = net.c, net.y, net.z
+    slot = net.slot()
+    net.start(pay.at[1 - c], pair, net.dev(c=1 - c), slot)
+    yield 3.0
+    net.arrive(pair, slot)
+
+    def add_pair(i, carry):
+        acc[i] = (pay[c, i].astype(F32) + pair[i].astype(F32)).astype(BF)
+        return carry
+
+    lax.fori_loop(0, NY, add_pair, 0)
+    near, over = y + 1 - 2 * lax.rem(y, 2), NY - 1 - y
+    half = NZ // 2
+    colors = []
+    for color, (f, s) in enumerate(((near, over), (over, near))):
+        s_of_f = lax.rem(y + 2, NY)
+        zs = pl.ds(color * half, half)
+        slots = [net.slot() for _ in range(3)]
+        net.start(acc.at[f, zs], got1.at[color, 0], net.dev(y=f), slots[0])
+        net.start(acc.at[s_of_f, zs], got1.at[color, 1], net.dev(y=f), slots[1])
+        colors.append((f, s, zs, slots))
+    yield 10.0
+    for color, (f, s, zs, slots) in enumerate(colors):
+        net.arrive(got1.at[color, 1], slots[1])
+        acc[s, zs] = (acc[s, zs].astype(F32) + got1[color, 1].astype(F32)).astype(BF)
+        net.start(acc.at[s, zs], got2.at[color], net.dev(y=s), slots[2])
+    yield 15.0
+    for color, (f, s, zs, slots) in enumerate(colors):
+        net.arrive(got1.at[color, 0], slots[0])
+        net.arrive(got2.at[color], slots[2])
+        acc[y, zs] = (acc[y, zs].astype(F32) + got1[color, 0].astype(F32) + got2[color].astype(F32)).astype(BF)
+    zslots = [net.slot() for _ in range(NZ - 1)]
+    for d in (4, 3, 5, 2, 6, 1, 7):
+        net.start(acc.at[y, net.at("z", d)], gotz.at[d - 1], net.dev(z=net.at("z", d)), zslots[d - 1])
+    yield 23.0
+    total = acc[y, z].astype(F32)
+    for d in range(1, NZ):
+        net.arrive(gotz.at[d - 1], zslots[d - 1])
+        total = total + gotz[d - 1].astype(F32)
+    xs_out[...] = total[keep_rows:]
+    xslots = [net.slot() for _ in range(3)]
+    for d in (1, 2, 3):
+        net.start(xs_out, xs_in.at[d - 1], net.dev(x=net.at("x", d)), xslots[d - 1])
+    yield 26.0
+    tail = total[keep_rows:]
+    for d in (1, 2, 3):
+        net.arrive(xs_in.at[d - 1], xslots[d - 1])
+    summed = tail + xs_in[0] + xs_in[1] + xs_in[2]
+    index = lax.broadcasted_iota(jnp.int32, tail.shape, 0)
+    tail = jnp.where(index < tail.shape[0] // 2, summed, tail)
+    whole[y, z, c] = jnp.concatenate([total[:keep_rows], tail], axis=0).astype(BF)
+    yield from gather_plane(net, whole, 16, 32, whole.shape[-1], 27.0, 0.35)
+
+
+def gather_rows(net, pi, pall):
+    rows = pi.shape[0] // 2
+    halves = (pl.ds(0, rows), pl.ds(rows, rows))
+    x = net.x
+    slots = {(d, i): net.slot() for d in (0, 1) for i in range(3)}
+    for i in (0, 1):
+        for d, way in ((0, 1), (1, -1)):
+            h = halves[i if d == 0 else 1 - i]
+            net.start(pi.at[h], pall.at[x, h], net.dev(x=net.at("x", way)), slots[d, i])
+    pall[x] = pi[...]
+    yield 13.0
+    for d, way in ((0, 1), (1, -1)):
+        ref = pall.at[net.at("x", -way), halves[d]]
+        net.arrive(ref, slots[d, 0])
+        net.start(ref, ref, net.dev(x=net.at("x", way)), slots[d, 2])
+    yield 36.0
+    for d, way in ((0, 1), (1, -1)):
+        net.arrive(pall.at[net.at("x", -way), halves[1 - d]], slots[d, 1])
+        net.arrive(pall.at[net.at("x", -2), halves[d]], slots[d, 2])
+
+
+def main_kernel(pi, blk, pay, pall, panel, whole, pair, acc, got1, got2, gotz, xs_out, xs_in, send, recv):
+    net = Net(send, recv)
+    peers = [net.dev(x=net.at("x", d)) for d in (1, 2, 3)]
+    peers += [net.dev(y=net.at("y", d)) for d in (1, 3)]
+    peers += [net.dev(z=net.at("z", d)) for d in range(1, NZ)]
+    peers += [net.dev(c=1 - net.c)]
+    net.greet(peers)
+    panel[net.y, net.z, net.c] = blk[...]
+    rows, lanes = blk.shape
+
+    def planes():
+        yield from gather_plane(net, panel, rows // 2, rows, lanes, 1.0, 1.1)
+
+    for _ in merge([
+        reduce_plane(net, pay, whole, pair, acc, got1, got2, gotz, xs_out, xs_in, 24),
+        gather_rows(net, pi, pall),
+        planes(),
+    ]):
+        pass
+    net.finish()
+
+
+def exchange(pi, blk, pay):
+    rows, lanes = blk.shape
+    vm = pl.BlockSpec(memory_space=pltpu.VMEM)
+    sems = 128
+    return pl.pallas_call(
+        main_kernel,
+        out_shape=[
+            jax.ShapeDtypeStruct((4, *pi.shape), BF),
+            jax.ShapeDtypeStruct((NY, NZ, 2, rows, lanes), BF),
+            jax.ShapeDtypeStruct((NY, NZ, 2, 32, lanes), BF),
+        ],
+        in_specs=[vm] * 3,
+        out_specs=[vm] * 3,
+        scratch_shapes=[
+            pltpu.VMEM((NY, NZ, 32, lanes), BF),
+            pltpu.VMEM((NY, NZ, 32, lanes), BF),
+            pltpu.VMEM((2, 2, NZ // 2, 32, lanes), BF),
+            pltpu.VMEM((2, NZ // 2, 32, lanes), BF),
+            pltpu.VMEM((NZ - 1, 32, lanes), BF),
+            pltpu.VMEM((8, lanes), F32),
+            pltpu.VMEM((3, 8, lanes), F32),
+            pltpu.SemaphoreType.DMA((sems,)),
+            pltpu.SemaphoreType.DMA((sems,)),
+        ],
+        compiler_params=pltpu.CompilerParams(collective_id=1, has_side_effects=True, vmem_limit_bytes=48 * 1024 * 1024),
+        name="exchange",
+    )(pi, blk, pay)
+
+
+def rows_kernel(blk, out, send, recv):
+    net = Net(send, recv)
+    net.greet([net.dev(x=net.at("x", d)) for d in (1, 2, 3)])
+    slots = [net.slot() for _ in range(3)]
+    lanes = blk.shape[1]
+
+    def place(x):
+        return out.at[:, pl.ds(pl.multiple_of(x * lanes, lanes), lanes)]
+
+    for d in (2, 1, 3):
+        net.start(blk, place(net.x), net.dev(x=net.at("x", d)), slots[d - 1])
+    out[:, pl.ds(pl.multiple_of(net.x * lanes, lanes), lanes)] = blk[...]
+    for d in (1, 3, 2):
+        net.arrive(place(net.at("x", -d)), slots[d - 1])
+    net.finish()
+
+
+def over_row(blk, ident):
+    vm = pl.BlockSpec(memory_space=pltpu.VMEM)
+    return pl.pallas_call(
+        rows_kernel,
+        out_shape=jax.ShapeDtypeStruct((blk.shape[0], 4 * blk.shape[1]), blk.dtype),
+        in_specs=[vm],
+        out_specs=vm,
+        scratch_shapes=[pltpu.SemaphoreType.DMA((3,)), pltpu.SemaphoreType.DMA((3,))],
+        compiler_params=pltpu.CompilerParams(collective_id=ident, has_side_effects=True, vmem_limit_bytes=4 * 1024 * 1024),
+        name="rows",
+    )(blk)
 
 
 def by_lead(x, gamma):
@@ -45,8 +324,7 @@
     rho_t = jnp.swapaxes(density, 1, 2).astype(BF).reshape(2 * cols, rows)
     ham_ct = jnp.swapaxes(lax.dynamic_slice_in_dim(hamiltonian, col_start, cols, 1), 0, 1)
 
-    first = over_row(jnp.concatenate([ham_ct, rho_t], axis=0))
-    first = jnp.moveaxis(first, 0, 1).reshape(3 * cols, n)
+    first = over_row(jnp.concatenate([ham_ct, rho_t], axis=0), 2)
     ham_c = first[:cols]
     applied = dot(first, hamiltonian, 1, 1)
     ham2_ct = applied[:cols].astype(BF)
@@ -56,10 +334,7 @@
     he_col = dot(ham_c, e_full).astype(BF)
     hg_col = by_lead(he_col, lead_gamma)
 
-    panel = lax.all_gather(rho_t.reshape(2, cols, rows), "mode", axis=1, tiled=True)
-    ham2_all = lax.all_gather(ham2_ct, "mode", axis=0, tiled=True)
     pi_b = auxiliary.astype(BF).reshape(rows, modes * 2 * coupled)
-    pi_all = lax.all_gather(pi_b, "row", axis=0, tiled=True)
 
     onehot = (lead_index[:, None] == jnp.arange(leads, dtype=jnp.int32)[None, :]).astype(F32)
     lam_re, lam_im = -mode_width, mode_level
@@ -87,19 +362,23 @@
     piece = rows // n_mode
     n_piece = q // n_mode
     scal = jnp.concatenate([w_l, v_l])
-    scal = jnp.zeros((n_mode, 1, 2 * q), F32).at[:, 0, : scal.shape[0]].set(scal)
+    scal = jnp.zeros((n_mode, 4, 2 * q), F32).at[:, 0, : scal.shape[0]].set(scal)
     payload = jnp.concatenate(
         [a.reshape(n_mode, -1, 2 * q) for a in (l_part, m_part, f_part, n_part)] + [scal], axis=1
-    )
-    mine = lax.psum_scatter(payload, "mode", scatter_dimension=0, tiled=True)[0]
-    n_mine = over_row(mine[3 * piece : 3 * piece + n_piece]).sum(0)
-    w_sum, v_sum = mine[-1, : 2 * leads], mine[-1, 2 * leads : 4 * leads]
-    mine = jnp.concatenate([mine[: 3 * piece], n_mine], axis=0).astype(BF)
-    whole = lax.all_gather(mine, "mode", axis=0, tiled=False)
+    ).astype(BF)
+    payload = payload.reshape(NY, NZ, 2, 32, 2 * q).transpose(2, 0, 1, 3, 4)
+    pi_all, panel, whole = exchange(pi_b, jnp.concatenate([rho_t, ham2_ct], 0), payload)
+    pi_all = pi_all.reshape(n, -1)
+    panel = panel.reshape(n_mode, 3, cols, rows)
+    ham2_all = panel[:, 2].reshape(n, rows)
+    panel = [panel[:, p].reshape(n, rows) for p in range(2)]
+    whole = whole.reshape(n_mode, 32, 2 * q)
     l1_b = whole[:, :piece].reshape(rows, 2 * q)
     m1 = whole[:, piece : 2 * piece].reshape(rows, 2 * q).astype(F32)
     f_all = whole[:, 2 * piece : 3 * piece].reshape(rows, 2 * q).astype(F32)
-    n_all = whole[:, 3 * piece :].reshape(q, 2 * q)
+    n_all = whole[:, 3 * piece : 3 * piece + n_piece].reshape(q, 2 * q)
+    scal = whole[0, 3 * piece + n_piece].astype(F32)
+    w_sum, v_sum = scal[: 2 * leads], scal[2 * leads : 4 * leads]
 
     grow_full = by_lead(e_full, lead_gamma).astype(BF)
     src = jnp.concatenate([dot(panel[p], grow_full, 0, 0) for p in range(2)], axis=1)
@@ -120,12 +399,12 @@
     own_l = lax.dynamic_slice_in_dim(l1_b, col_start - owner * rows, cols, 0)
     own_x = lax.dynamic_slice_in_dim(x_row, col_start - owner * rows, cols, 0)
     mask = (x_pos == owner).astype(BF)
-    second = over_row(jnp.concatenate([y.astype(BF), ham2_ct], 0))
-    second = jnp.moveaxis(second, 0, 1).reshape(3 * cols, n)
-    third = over_row(jnp.concatenate([z.astype(BF), own_l * mask, own_x * mask], 0)).astype(F32).sum(0)
+    second = over_row(jnp.concatenate([y.astype(BF), ham2_ct, z.astype(BF), own_l * mask, own_x * mask], 0), 3)
+    third = second[3 * cols :].astype(F32)
+    third = sum(third[:, i * rows : (i + 1) * rows] for i in range(n_row))
     z, l_c, x_c = third[:cols], third[cols : 2 * cols], third[2 * cols :]
     hy = dot(second[: 2 * cols], hamiltonian, 1, 1)
-    ham2_c = second[2 * cols :]
+    ham2_c = second[2 * cols : 3 * cols]
     rhoh2_t = jnp.concatenate([dot(ham2_c, panel[p]) for p in range(2)], 0)
     b_re = x_c[:, :q] + 4 * H2 * z[:, q:]
     b_im = -x_c[:, q:] + 4 * H2 * z[:, :q]

time: 599 us -> 319 us (0.53)
  waiting for transfers between devices: 329 us -> 0 us
  Pallas kernels: 0 us -> 99.6 us
  local copies, waits for them, and re-layouts: 86.9 us -> 69.7 us
  starting transfers between devices: 17.1 us -> 0 us
  between operations: 45.6 us -> 32.2 us
  matrix products: 42.4 us -> 34.2 us
    all_gather x4 -> x0, waiting for transfers between devices: 228 us -> none  [the longest x1 74 us: shards(): ham2_all = lax.all_gather(ham2_ct, 'mode', axis=0, tiled=True)]
    pallas_call x0 -> x3, Pallas kernels: none -> 99.6 us  [the longest x1 77.6 us: exchange(): pl.pallas_call(main_kernel, out_shape=[jax.ShapeDtypeStruct((4, *pi.shape...]
    reduce_scatter x1 -> x0, waiting for transfers between devices: 96.6 us -> none  [shards(): mine = lax.psum_scatter(payload, 'mode', scatter_dimension=0, tiled=True)[0]]
    add x5 -> x0, other arithmetic: 39.9 us -> none  [the longest x2 16.9 us: shards(): sum((onehot[k, l] * (lam_re[k] * auxiliary[:, k, 0] - lam_im[k] * auxilia...]
    another operation x1 -> x7, other arithmetic: 0.02 us -> 36.2 us
    all_to_all x4 -> x0, starting transfers between devices: 17 us -> none  [over_row(): lax.all_to_all(jnp.broadcast_to(x[None], (devices, *x.shape)), 'row', 0,...]
    unnamed x204 -> x149, local copies, waits for them, and re-layouts: 38 us -> 22.1 us
    unnamed x6 -> x8, other arithmetic: 8.78 us -> 20.8 us
  transfers between devices with their start and end apart: 9 -> 0, of which waited for: 6 -> 0; matrix products, arithmetic and copies ran while one was open for 27% -> 0% of each run, Pallas kernels for 0% -> 0%
where the time goes in v1:
time: 319 us; the launch traced here: 316 us
  Pallas kernels  99.6 us (31%)
  other arithmetic  80.2 us (25%)
  local copies, waits for them, and re-layouts  69.7 us (22%)
  matrix products  34.2 us (11%)
  between operations  32.2 us (10%)
    pallas_call x1, Pallas kernels, exchange(): pl.pallas_call(main_kernel, out_shape=[jax.ShapeDtypeStruct((4, *pi.shape...  77.6 us
    another operation x7, other arithmetic  36.2 us
    dot_general x42, matrix products, dot(): lax.dot_general(a, b, (((ca,), (cb,)), ((), ())), preferred_element_type=...  34.2 us
    unnamed x149, local copies, waits for them, and re-layouts  22.1 us
    pallas_call x2, Pallas kernels, over_row(): pl.pallas_call(rows_kernel, out_shape=jax.ShapeDtypeStruct((blk.shape[0],...  22 us
    unnamed x8, other arithmetic  20.8 us
    concatenate x5, local copies, waits for them, and re-layouts, shards(): jnp.concatenate([a.reshape(n_mode, -1, 2 * q) for a in (l_part, m_part, f...  18.8 us
    sub x3, other arithmetic, shards(): br, bi = (sr - occ * gk, si - occ * gk)  10.5 us

profile of v1, /device:TPU:1, one launch (start us, length us, event | category | flops | bytes accessed | tf_op | source)
XLA Modules:
  0.0 315.9 jit_solution(5208266580769983391)
XLA Ops:
  2.2 2.2 convolution_convert_fusion.4
  6.1 1.8 reshape.535.pi
  8.6 9.2 %rows.2 = bf16[96,2048]{1,0:T(8,128)(2,1)S(1)} custom-call(bf16[96,512]{1,0:T(8,128)(2,1)S(1)} %pad_maximum_fusion.9.blk), custom_call_target="tpu_custom_call" | custom-call | tf_op jit(solution)/shard_map/rows/pallas_call | solution.py:288
  21.8 5.2 %add_convert_fusion.5 = (bf16[512,1,1,128]{3,0,2,1:T(8,128)(2,1)S(1)}, bf16[512,1,1,128]{3,0,2,1:T(8,128)(2,1)S(1)}, bf16[512,1,1,128]{3,0,2,1:T(8,128)(2,1)S(1)}, bf16[512,1,1,128]{3,0,2,1:T(8,128)(2,1)S(1)}) fusion(f32[512,1,1,128]{3,0,2,1:T(8,128)S(1)} %bitcast.322, f32[512,1,1,128]{3,0,2,1:T(8,128)S(1)} %bitcast.329, ...), kind=kLoop, calls=%fused_computation.170 | loop fusion | flops 2097152 | bytes 2621472 | tf_op jit(solution)/shard_map/convert.25
  29.4 7.7 %add_convert_fusion = bf16[512,1,1,128]{3,0,2,1:T(8,128)(2,1)S(1)} fusion(f32[]{:T(128)} %bitcast.12, f32[]{:T(128)} %bitcast.11, f32[]{:T(128)} %bitcast.10, f32[]{:T(128)} %bitcast.9, f32[512,1,1,128]{3,0,2,1:T(8,128)S(1)} %bitcast.302, f32[]{:T(128)} %bitcast.17, f32[512,1,1,128]{3,0,2,1:T(8,128)S(1)} %bitcast.309, f32[]{:T(128)} %bitcast.16, ...), kind=kLoop, calls=%fused_computation.128 | loop fusion | flops 1310720 | bytes 2228272 | tf_op jit(solution)/shard_map/convert.19
  37.1 7.7 %add_convert_fusion.1 = bf16[512,1,1,128]{3,0,2,1:T(8,128)(2,1)S(1)} fusion(f32[]{:T(128)} %bitcast.7, f32[]{:T(128)} %bitcast.6, f32[]{:T(128)} %bitcast.5, f32[]{:T(128)} %bitcast.4, f32[512,1,1,128]{3,0,2,1:T(8,128)S(1)} %bitcast.303, f32[]{:T(128)} %bitcast.17, f32[512,1,1,128]{3,0,2,1:T(8,128)S(1)} %bitcast.310, f32[]{:T(128)} %bitcast.16, ...), kind=kLoop, calls=%fused_computation.129 | loop fusion | flops 1310720 | bytes 2228272 | tf_op jit(solution)/shard_map/convert.18
  44.8 7.7 %add_convert_fusion.2 = bf16[512,1,1,128]{3,0,2,1:T(8,128)(2,1)S(1)} fusion(f32[]{:T(128)} %bitcast.12, f32[]{:T(128)} %bitcast.11, f32[]{:T(128)} %bitcast.10, f32[]{:T(128)} %bitcast.9, f32[512,1,1,128]{3,0,2,1:T(8,128)S(1)} %bitcast.311, f32[]{:T(128)} %bitcast.17, f32[512,1,1,128]{3,0,2,1:T(8,128)S(1)} %bitcast.304, f32[]{:T(128)} %bitcast.16, ...), kind=kLoop, calls=%fused_computation.130 | loop fusion | flops 1310720 | bytes 2228272 | tf_op jit(solution)/shard_map/convert.17
  52.6 7.7 %add_convert_fusion.3 = bf16[512,1,1,128]{3,0,2,1:T(8,128)(2,1)S(1)} fusion(f32[]{:T(128)} %bitcast.7, f32[]{:T(128)} %bitcast.6, f32[]{:T(128)} %bitcast.5, f32[]{:T(128)} %bitcast.4, f32[512,1,1,128]{3,0,2,1:T(8,128)S(1)} %bitcast.312, f32[]{:T(128)} %bitcast.17, f32[512,1,1,128]{3,0,2,1:T(8,128)S(1)} %bitcast.305, f32[]{:T(128)} %bitcast.16, ...), kind=kLoop, calls=%fused_computation.131 | loop fusion | flops 1310720 | bytes 2228272 | tf_op jit(solution)/shard_map/convert.16
  64.3 2.0 copy.110
  66.3 1.9 copy.114
  74.3 1.8 copy.113
  82.7 12.7 %concatenate.117 = bf16[4,8,2,32,512]{4,3,1,0,2:T(8,128)(2,1)} concatenate(bf16[4,8,2,8,512]{4,3,1,0,2:T(8,128)(2,1)} %copy.149, bf16[4,8,2,8,512]{4,3,1,0,2:T(8,128)(2,1)} %copy.150, bf16[4,8,2,8,512]{4,3,1,0,2:T(8,128)(2,1)} %copy.114, bf16[4,8,2,4,512]{4,3,1,0,2:T(4,128)(2,1)} %copy.115, bf16[4,8,2,4,512]{4,3,1,0,2:T(4,128)(2,1)} %concatenate.116), dimensions={3} | concatenate | bytes 4194304 | tf_op jit(solution)/shard_map/concatenate | solution.py:366
  97.9 77.6 %exchange.1 = (bf16[4,512,1024]{2,1,0:T(8,128)(2,1)}, bf16[4,8,2,96,512]{4,3,2,1,0:T(8,128)(2,1)}, bf16[4,8,2,32,512]{4,3,2,1,0:T(8,128)(2,1)S(1)}) custom-call(bf16[512,1024]{1,0:T(8,128)(2,1)S(1)} %reshape.535.pi, bf16[96,512]{1,0:T(8,128)(2,1)S(1)} %copy-done.4, bf16[2,4,8,32,512]{4,3,2,1,0:T(8,128)(2,1)S(1)} %bitcast.288), custom_call_target="tpu_custom_call" | custom-call | tf_op jit(solution)/shard_map/exchange/pallas_call | solution.py:244
  176.0 5.6 %fusion.207 = (bf16[64,1,32,512]{3,2,1,0:T(8,128)(2,1)}, bf16[64,1,32,512]{3,2,1,0:T(8,128)(2,1)S(1)}, bf16[64,1,32,512]{3,2,1,0:T(8,128)(2,1)S(1)}) fusion(bf16[64,3,32,512]{3,2,1,0:T(8,128)(2,1)} %bitcast.357), kind=kLoop, calls=%fused_computation.338 | loop fusion | bytes 12582912 | tf_op jit(solution)/shard_map/slice | solution.py:373
  192.2 12.8 %rows.3 = bf16[192,2048]{1,0:T(8,128)(2,1)S(1)} custom-call(bf16[192,512]{1,0:T(8,128)(2,1)S(1)} %multiply_dynamic-update-slice_fusion.blk), custom_call_target="tpu_custom_call" | custom-call | tf_op jit(solution)/shard_map/rows/pallas_call | solution.py:288
  209.2 6.5 %copy.123 = bf16[1024,2048]{1,0:T(8,128)(2,1)} copy(bf16[1024,2048]{0,1:T(8,128)(2,1)} %bitcast.358) | data formatting | bytes 8388608 | tf_op jit(solution)/shard_map/dot_general | solution.py:14
  215.7 6.7 %fusion.218 = f32[512,4,2,128]{3,0,2,1:T(8,128)} fusion(bf16[2048,512,1,1]{1,0,3,2:T(8,128)(2,1)} %bitcast.366, bf16[4,2,128,2048]{3,2,1,0:T(8,128)(2,1)} %bitcast.360), kind=kOutput, calls=%fused_computation.349 | convolution fusion | flops 2147483648 | bytes 8388608 | tf_op jit(solution)/shard_map/dot_general | solution.py:14
  222.4 2.4 fusion.217
  236.2 2.4 fusion
  240.4 2.7 select_subtract_fusion.7
  244.3 4.1 %fusion.72 = (f32[512,8,128]{2,0,1:T(8,128)}, f32[512,128]{1,0:T(8,128)S(1)}, f32[512,128]{1,0:T(8,128)S(1)}, f32[512,128]{1,0:T(8,128)}) fusion(f32[512,4,2,128]{3,0,2,1:T(8,128)} %fusion.218, f32[512,1,1,128]{3,0,2,1:T(8,128)} %copy.162, f32[512,1,1,128]{3,0,2,1:T(8,128)} %copy.161, f32[512,1,1,128]{3,0,2,1:T(8,128)S(1)} %bitcast.313, ...), kind=kOutput, calls=%fused_computation.115 | convolution fusion | flops 18546688 | bytes 4359197 | tf_op jit(solution)/shard_map/dot_general | solution.py:14
  248.4 3.1 fusion.66
  253.3 1.8 copy.164
  263.1 3.9 %select_subtract_fusion = (f32[512,128]{1,0:T(8,128)}, f32[512,128]{1,0:T(8,128)}, f32[512,128]{1,0:T(8,128)}) fusion(f32[512,256]{1,0:T(8,128)} %get-tuple-element.119, pred[]{:T(512)S(6)} %gt.15, f32[512,256]{1,0:T(8,128)S(1)} %fusion.205, f32[]{:T(128)} %bitcast.92, f32[]{:T(128)} %bitcast.85, pred[]{:T(512)S(6)} %gt.14, f32[]{:T(128)} %bitcast.78, ...), kind=kLoop, calls=%fused_computation.135 | loop fusion | flops 786432 | bytes 1835023 | tf_op jit(solution)/shard_map/sub | solution.py:439
  267.6 3.8 %select_subtract_fusion.1 = (f32[512,128]{1,0:T(8,128)}, f32[512,128]{1,0:T(8,128)}, f32[512,128]{1,0:T(8,128)}) fusion(f32[512,256]{1,0:T(8,128)} %copy-done.35, pred[]{:T(512)S(6)} %gt.15, f32[512,256]{1,0:T(8,128)S(1)} %fusion.205, f32[]{:T(128)} %bitcast.92, f32[]{:T(128)} %bitcast.85, pred[]{:T(512)S(6)} %gt.14, f32[]{:T(128)} %bitcast.78, pred[]{:T(512)S(6)} %gt.13), kind=kLoop, calls=%fused_computation.137 | loop fusion | flops 786432 | bytes 1835023 | tf_op jit(solution)/shard_map/sub | solution.py:439
  272.2 4.0 %fusion.60 = (f32[512,8,128]{2,0,1:T(8,128)}, f32[512,128]{1,0:T(8,128)S(1)}, f32[512,128]{1,0:T(8,128)S(1)}) fusion(f32[512,8,128]{2,0,1:T(8,128)} %fusion.66, f32[512,4,2,128]{3,0,2,1:T(8,128)} %fusion.218, f32[512,1,1,128]{3,0,2,1:T(8,128)} %copy.165, f32[512,1,1,128]{3,0,2,1:T(8,128)} %copy.164, f32[512,1,1,128]{3,0,2,1:T(8,128)S(1)} %bitcast.348, ...), kind=kLoop, calls=%fused_computation.101 | loop fusion | flops 1769472 | bytes 4195357
  276.2 3.2 fusion.54
  288.5 3.6 %fusion.48 = (f32[512,8,128]{2,0,1:T(8,128)}, f32[512,128]{1,0:T(8,128)S(1)}, f32[512,128]{1,0:T(8,128)S(1)}) fusion(f32[512,8,128]{2,0,1:T(8,128)} %fusion.54, f32[512,4,2,128]{3,0,2,1:T(8,128)} %fusion.218, f32[512,1,1,128]{3,0,2,1:T(8,128)S(1)} %copy.167, f32[512,1,1,128]{3,0,2,1:T(8,128)S(1)} %copy.166, f32[512,1,1,128]{3,0,2,1:T(8,128)S(1)} %bitcast.334, ...), kind=kLoop, calls=%fused_computation.87 | loop fusion | flops 1769472 | bytes 4195357
  292.1 3.2 %fusion.42 = f32[512,8,128]{2,0,1:T(8,128)} fusion(f32[512,8,128]{2,0,1:T(8,128)} %get-tuple-element.33, f32[512,4,2,128]{3,0,2,1:T(8,128)} %fusion.218, f32[512,128]{1,0:T(8,128)S(1)} %get-tuple-element.34, f32[512,128]{1,0:T(8,128)S(1)} %get-tuple-element.35, f32[512,1,1,128]{3,0,2,1:T(8,128)} %copy-done.34, f32[512,1,1,128]{3,0,2,1:T(8,128)} %copy-done.33, ...), kind=kLoop, calls=%fused_computation.80 | loop fusion | flops 851968 | bytes 2098192
  304.8 3.6 %fusion.36 = (f32[512,8,128]{2,0,1:T(8,128)}, f32[512,128]{1,0:T(8,128)S(1)}, f32[512,128]{1,0:T(8,128)S(1)}) fusion(f32[512,8,128]{2,0,1:T(8,128)} %fusion.42, f32[512,4,2,128]{3,0,2,1:T(8,128)} %fusion.218, f32[512,1,1,128]{3,0,2,1:T(8,128)S(1)} %copy.169, f32[512,1,1,128]{3,0,2,1:T(8,128)S(1)} %copy.168, f32[512,1,1,128]{3,0,2,1:T(8,128)S(1)} %bitcast.327, ...), kind=kLoop, calls=%fused_computation.73 | loop fusion | flops 1769472 | bytes 4195357
  308.4 3.0 fusion.30
  311.4 4.5 %copy.139 = f32[512,4,2,128]{3,2,1,0:T(2,128)} copy(f32[512,4,2,128]{3,0,2,1:T(8,128)} %bitcast.361) | data formatting | bytes 4194304
  (242 shorter events, 57.6 us)
Async XLA Ops:
  8.1 11.2 %copy-start.26 = (f32[512,4,2,128]{3,2,1,0:T(2,128)S(1)}, f32[512,4,2,128]{3,2,1,0:T(2,128)}, u32[]{:S(2)}) copy-start(f32[512,4,2,128]{3,2,1,0:T(2,128)} %param.13) | copy-start | bytes 6291460
  8.6 10.1 %copy-start.41 = (bf16[2,512,32]{1,2,0:T(8,128)(2,1)S(1)}, bf16[2,512,32]{1,2,0:T(8,128)(2,1)}, u32[]{:S(2)}) copy-start(bf16[2,512,32]{1,2,0:T(8,128)(2,1)} %copy-done.40) | copy-start | bytes 196612
  18.6 42.7 %copy-start.36 = (f32[96,512]{1,0:T(8,128)}, f32[96,512]{1,0:T(8,128)S(1)}, u32[]{:S(2)}) copy-start(f32[96,512]{1,0:T(8,128)S(1)} %fusion.216) | copy-start | bytes 589828
  20.9 31.6 %copy-start.9 = (f32[512,1,1,128]{3,2,1,0:T(1,128)}, f32[512,1,1,128]{3,2,1,0:T(1,128)S(1)}, u32[]{:S(2)}) copy-start(f32[512,1,1,128]{3,2,1,0:T(1,128)S(1)} %get-tuple-element.55) | copy-start | bytes 786436
  20.9 31.6 %copy-start.11 = (f32[512,1,1,128]{3,2,1,0:T(1,128)}, f32[512,1,1,128]{3,2,1,0:T(1,128)S(1)}, u32[]{:S(2)}) copy-start(f32[512,1,1,128]{3,2,1,0:T(1,128)S(1)} %get-tuple-element.58) | copy-start | bytes 786436
  20.9 31.6 %copy-start.13 = (f32[512,1,1,128]{3,2,1,0:T(1,128)}, f32[512,1,1,128]{3,2,1,0:T(1,128)S(1)}, u32[]{:S(2)}) copy-start(f32[512,1,1,128]{3,2,1,0:T(1,128)S(1)} %get-tuple-element.59) | copy-start | bytes 786436
  20.9 31.6 %copy-start.15 = (f32[512,1,1,128]{3,2,1,0:T(1,128)}, f32[512,1,1,128]{3,2,1,0:T(1,128)S(1)}, u32[]{:S(2)}) copy-start(f32[512,1,1,128]{3,2,1,0:T(1,128)S(1)} %get-tuple-element.62) | copy-start | bytes 786436
  20.9 31.6 %copy-start.17 = (f32[512,1,1,128]{3,2,1,0:T(1,128)}, f32[512,1,1,128]{3,2,1,0:T(1,128)S(1)}, u32[]{:S(2)}) copy-start(f32[512,1,1,128]{3,2,1,0:T(1,128)S(1)} %get-tuple-element.56) | copy-start | bytes 786436
  20.9 31.6 %copy-start.19 = (f32[512,1,1,128]{3,2,1,0:T(1,128)}, f32[512,1,1,128]{3,2,1,0:T(1,128)S(1)}, u32[]{:S(2)}) copy-start(f32[512,1,1,128]{3,2,1,0:T(1,128)S(1)} %get-tuple-element.60) | copy-start | bytes 786436
  20.9 31.6 %copy-start.21 = (f32[512,1,1,128]{3,2,1,0:T(1,128)}, f32[512,1,1,128]{3,2,1,0:T(1,128)S(1)}, u32[]{:S(2)}) copy-start(f32[512,1,1,128]{3,2,1,0:T(1,128)S(1)} %get-tuple-element.57) | copy-start | bytes 786436
  20.9 31.6 %copy-start.23 = (f32[512,1,1,128]{3,2,1,0:T(1,128)}, f32[512,1,1,128]{3,2,1,0:T(1,128)S(1)}, u32[]{:S(2)}) copy-start(f32[512,1,1,128]{3,2,1,0:T(1,128)S(1)} %get-tuple-element.61) | copy-start | bytes 786436
  21.8 6.9 %copy-start.68 = (f32[4]{0:T(128)S(1)}, f32[4]{0:T(128)}, u32[]{:S(2)}) copy-start(f32[4]{0:T(128)} %param.18) | copy-start | bytes 52
  27.0 10.0 %copy-start.46 = (bf16[512,1,1,128]{3,0,2,1:T(8,128)(2,1)}, bf16[512,1,1,128]{3,0,2,1:T(8,128)(2,1)S(1)}, u32[]{:S(2)}) copy-start(bf16[512,1,1,128]{3,0,2,1:T(8,128)(2,1)S(1)} %get-tuple-element.121) | copy-start | bytes 393220
  27.1 10.0 %copy-start.47 = (bf16[512,1,1,128]{3,0,2,1:T(8,128)(2,1)}, bf16[512,1,1,128]{3,0,2,1:T(8,128)(2,1)S(1)}, u32[]{:S(2)}) copy-start(bf16[512,1,1,128]{3,0,2,1:T(8,128)(2,1)S(1)} %get-tuple-element.122) | copy-start | bytes 393220
  27.1 10.0 %copy-start.48 = (bf16[512,1,1,128]{3,0,2,1:T(8,128)(2,1)}, bf16[512,1,1,128]{3,0,2,1:T(8,128)(2,1)S(1)}, u32[]{:S(2)}) copy-start(bf16[512,1,1,128]{3,0,2,1:T(8,128)(2,1)S(1)} %get-tuple-element.73) | copy-start | bytes 393220
  27.1 10.0 %copy-start.49 = (bf16[512,1,1,128]{3,0,2,1:T(8,128)(2,1)}, bf16[512,1,1,128]{3,0,2,1:T(8,128)(2,1)S(1)}, u32[]{:S(2)}) copy-start(bf16[512,1,1,128]{3,0,2,1:T(8,128)(2,1)S(1)} %get-tuple-element.74) | copy-start | bytes 393220
  52.6 8.7 %copy-start.45 = (f32[2,512,32]{1,2,0:T(8,128)S(1)}, f32[2,512,32]{1,2,0:T(8,128)}, u32[]{:S(2)}) copy-start(f32[2,512,32]{1,2,0:T(8,128)} %param.12) | copy-start | bytes 393220
  52.6 8.8 %copy-start.54 = (s32[2,128]{1,0:T(2,128)S(1)}, s32[2,128]{1,0:T(2,128)}, u32[]{:S(2)}) copy-start(s32[2,128]{1,0:T(2,128)} %param.15) | copy-start | bytes 3076
  97.9 77.7 %copy-start.55 = (s32[2,128]{1,0:T(2,128)S(1)}, s32[2,128]{1,0:T(2,128)}, u32[]{:S(2)}) copy-start(s32[2,128]{1,0:T(2,128)} %param.15) | copy-start | bytes 3076
  97.9 77.7 %copy-start.63 = (s32[32]{0:T(128)S(1)}, s32[32]{0:T(128)}, u32[]{:S(2)}) copy-start(s32[32]{0:T(128)} %copy-done.62) | copy-start | bytes 388
  192.1 13.0 %copy-start.30 = (bf16[256,512]{1,0:T(8,128)(2,1)S(1)}, bf16[256,512]{1,0:T(8,128)(2,1)}, u32[]{:S(2)}) copy-start(bf16[256,512]{1,0:T(8,128)(2,1)} %convolution_convert_fusion.4) | copy-start | bytes 786436
  224.8 8.3 %copy-start.65 = (f32[4]{0:T(128)S(1)}, f32[4]{0:T(128)}, u32[]{:S(2)}) copy-start(f32[4]{0:T(128)} %param.20) | copy-start | bytes 52
  226.0 10.2 %copy-start.57 = (s32[2,128]{1,0:T(2,128)S(1)}, s32[2,128]{1,0:T(2,128)}, u32[]{:S(2)}) copy-start(s32[2,128]{1,0:T(2,128)} %param.15) | copy-start | bytes 3076
  226.0 10.2 %copy-start.61 = (s32[512]{0:T(512)S(1)}, s32[512]{0:T(512)}, u32[]{:S(2)}) copy-start(s32[512]{0:T(512)} %copy-done.59) | copy-start | bytes 6148
  253.3 18.9 %copy-start.22 = (f32[512,1,1,128]{3,2,1,0:T(1,128)S(1)}, f32[512,1,1,128]{3,2,1,0:T(1,128)}, u32[]{:S(2)}) copy-start(f32[512,1,1,128]{3,2,1,0:T(1,128)} %copy-done.21) | copy-start | bytes 786436
  253.3 18.9 %copy-start.24 = (f32[512,1,1,128]{3,2,1,0:T(1,128)S(1)}, f32[512,1,1,128]{3,2,1,0:T(1,128)}, u32[]{:S(2)}) copy-start(f32[512,1,1,128]{3,2,1,0:T(1,128)} %copy-done.23) | copy-start | bytes 786436
  276.2 12.3 %copy-start.18 = (f32[512,1,1,128]{3,2,1,0:T(1,128)S(1)}, f32[512,1,1,128]{3,2,1,0:T(1,128)}, u32[]{:S(2)}) copy-start(f32[512,1,1,128]{3,2,1,0:T(1,128)} %copy-done.17) | copy-start | bytes 786436
  276.2 12.3 %copy-start.20 = (f32[512,1,1,128]{3,2,1,0:T(1,128)S(1)}, f32[512,1,1,128]{3,2,1,0:T(1,128)}, u32[]{:S(2)}) copy-start(f32[512,1,1,128]{3,2,1,0:T(1,128)} %copy-done.19) | copy-start | bytes 786436
  280.5 8.0 %copy-start.33 = (f32[512,1,1,128]{3,0,2,1:T(8,128)}, f32[512,1,1,128]{3,0,2,1:T(8,128)S(1)}, u32[]{:S(2)}) copy-start(f32[512,1,1,128]{3,0,2,1:T(8,128)S(1)} %copy.167) | copy-start | bytes 786436
  281.6 6.8 %copy-start.34 = (f32[512,1,1,128]{3,0,2,1:T(8,128)}, f32[512,1,1,128]{3,0,2,1:T(8,128)S(1)}, u32[]{:S(2)}) copy-start(f32[512,1,1,128]{3,0,2,1:T(8,128)S(1)} %copy.166) | copy-start | bytes 786436
  292.1 12.6 %copy-start.14 = (f32[512,1,1,128]{3,2,1,0:T(1,128)S(1)}, f32[512,1,1,128]{3,2,1,0:T(1,128)}, u32[]{:S(2)}) copy-start(f32[512,1,1,128]{3,2,1,0:T(1,128)} %copy-done.13) | copy-start | bytes 786436
  292.1 12.6 %copy-start.16 = (f32[512,1,1,128]{3,2,1,0:T(1,128)S(1)}, f32[512,1,1,128]{3,2,1,0:T(1,128)}, u32[]{:S(2)}) copy-start(f32[512,1,1,128]{3,2,1,0:T(1,128)} %copy-done.15) | copy-start | bytes 786436
  (37 other events, 99.8 us)

commit v2 on v1

--- a/solution.py
+++ b/solution.py
@@ -188,8 +188,7 @@
     for d in (1, 2, 3):
         net.arrive(xs_in.at[d - 1], xslots[d - 1])
     summed = tail + xs_in[0] + xs_in[1] + xs_in[2]
-    index = lax.broadcasted_iota(jnp.int32, tail.shape, 0)
-    tail = jnp.where(index < tail.shape[0] // 2, summed, tail)
+    tail = jnp.where(jnp.full(tail.shape, c) == 0, summed, tail)
     whole[y, z, c] = jnp.concatenate([total[:keep_rows], tail], axis=0).astype(BF)
     yield from gather_plane(net, whole, 16, 32, whole.shape[-1], 27.0, 0.35)
 
@@ -296,6 +295,132 @@
     )(blk)
 
 
+def sums_kernel(lead, coef, aux, f_re, f_im, g_row, pi, pay, held):
+    q = g_row.shape[1]
+    coupled = aux.shape[1]
+    modes = aux.shape[0] // (2 * held.shape[0])
+    leads = q // coupled
+    hot = [[jnp.where(lead[k] == l, 1.0, 0.0) for l in range(leads)] for k in range(modes)]
+    level, width, re, im, occ = ([coef[i, k] for k in range(modes)] for i in range(5))
+
+    def chunk(t, carry):
+        rows = pl.ds(pl.multiple_of(32 * t, 32), 32)
+        part = [aux[pl.ds(pl.multiple_of(32 * t * 2 * modes, 32) + i, 32, stride=2 * modes), :] for i in range(2 * modes)]
+        pi[rows, :] = jnp.concatenate(part, axis=1).astype(BF)
+        turned = []
+        for k in range(modes):
+            turned.append(-width[k] * part[2 * k] - level[k] * part[2 * k + 1])
+            turned.append(level[k] * part[2 * k] - width[k] * part[2 * k + 1])
+
+        def summed(values):
+            out = []
+            for p in range(2):
+                for l in range(leads):
+                    total = hot[0][l] * values[p]
+                    for k in range(1, modes):
+                        total = total + hot[k][l] * values[2 * k + p]
+                    out.append(total)
+            return jnp.concatenate(out, axis=1)
+
+        l_sum = summed(part)
+        held[rows, :] = l_sum.astype(BF)
+        f = jnp.concatenate([f_re[rows, :], f_im[rows, :]], axis=1)
+        for i, a in enumerate((l_sum, summed(turned), f)):
+            a = a.reshape(2, 2, 8, 2 * q).astype(BF)
+            for c in range(2):
+                pay[c, t // 4, pl.ds(2 * lax.rem(t, 4), 2), pl.ds(8 * i, 8), :] = a[:, c]
+        return carry
+
+    lax.fori_loop(0, pi.shape[0] // 32, chunk, 0)
+    n_re = dot(held[:, :q], g_row[...], 0, 0)
+    n_im = -dot(held[:, q:], g_row[...], 0, 0)
+    n = jnp.concatenate([n_re, n_im], axis=1).astype(BF)
+    pay[0, :, :, 24:32, :] = n.reshape(NY, NZ, 8, 2 * q)
+    lane = lax.broadcasted_iota(jnp.int32, (8, 2 * q), 1)
+    scal = jnp.zeros((8, 2 * q), F32)
+    for i, weights in enumerate((re, im, [re[k] * occ[k] for k in range(modes)], [im[k] * occ[k] for k in range(modes)])):
+        for l in range(leads):
+            scal = jnp.where(lane == i * leads + l, sum(weights[k] * hot[k][l] for k in range(modes)), scal)
+    pay[1, :, :, 24:32, :] = jnp.broadcast_to(scal.astype(BF), (NY, NZ, 8, 2 * q))
+
+
+def local_sums(lead, coef, aux, f_re, f_im, g_row):
+    rows, q = g_row.shape
+    vm = pl.BlockSpec(memory_space=pltpu.VMEM)
+    sm = pl.BlockSpec(memory_space=pltpu.SMEM)
+    return pl.pallas_call(
+        sums_kernel,
+        out_shape=[
+            jax.ShapeDtypeStruct((rows, aux.size // rows), BF),
+            jax.ShapeDtypeStruct((2, NY, NZ, 32, 2 * q), BF),
+        ],
+        in_specs=[sm, sm, vm, vm, vm, vm],
+        out_specs=[vm, vm],
+        scratch_shapes=[pltpu.VMEM((rows, 2 * q), BF)],
+        compiler_params=pltpu.CompilerParams(vmem_limit_bytes=24 * 1024 * 1024),
+        name="sums",
+    )(lead, coef, aux, f_re, f_im, g_row)
+
+
+def modes_kernel(lead, coef, aux, ham, ham2, pi, src, u, g, hg, out, hp, h2p):
+    k = pl.program_id(0)
+    coupled = aux.shape[1]
+    rows = ham.shape[0]
+    modes = aux.shape[0] // (2 * rows)
+    q = g.shape[1]
+    hp[...] = dot(ham[...], pi[...])
+    h2p[...] = dot(ham2[...], pi[...])
+    level, width, wr, wi, occ = (coef[i, k] for i in range(5))
+    first = pl.multiple_of(lead[k] * coupled, coupled)
+    re, im = pl.ds(first, coupled), pl.ds(pl.multiple_of(q + first, coupled), coupled)
+    lr, li = -width, level
+    ar, ai = 3 + 2 * H2 * lr, 2 * H2 * li
+    cr = 3 * lr + 2 * H2 * (lr * lr - li * li)
+    ci = 3 * li + 4 * H2 * lr * li
+    er, ei = 4 * H2 * li, -3 - 4 * H2 * lr
+    size = 64
+
+    def chunk(t, carry):
+        at = pl.ds(pl.multiple_of(size * t, size), size)
+        gk, hgk = occ * g[at, re].astype(F32), 2 * H2 * occ * hg[at, re]
+        br, bi = src[at, re] - gk, src[at, im] - gk
+        tr = ar * br - ai * bi + u[at, re] - hgk
+        ti = ar * bi + ai * br + u[at, im] + hgk
+        start = pl.multiple_of(size * t * 2 * modes, size) + 2 * k
+        at_re = pl.ds(start, size, stride=2 * modes)
+        at_im = pl.ds(start + 1, size, stride=2 * modes)
+        pr, pim = aux[at_re, :], aux[at_im, :]
+        hr, hi = hp[at, :coupled], hp[at, coupled:]
+        out[at_re, :] = cr * pr - ci * pim + er * hr - ei * hi - 2 * H2 * h2p[at, :coupled] + wr * tr - wi * ti
+        out[at_im, :] = cr * pim + ci * pr + er * hi + ei * hr - 2 * H2 * h2p[at, coupled:] + wr * ti + wi * tr
+        return carry
+
+    lax.fori_loop(0, rows // size, chunk, 0)
+
+
+def advance_modes(lead, coef, aux, ham, ham2, pi, src, u, g, hg):
+    rows, n = ham.shape
+    coupled = aux.shape[1]
+    modes = aux.shape[0] // (2 * rows)
+    sm = pl.BlockSpec(memory_space=pltpu.SMEM)
+
+    def whole(a):
+        return pl.BlockSpec(a.shape, lambda k: (0,) * a.ndim)
+
+    return pl.pallas_call(
+        modes_kernel,
+        grid=(modes,),
+        out_shape=jax.ShapeDtypeStruct(aux.shape, F32),
+        in_specs=[sm, sm, whole(aux), whole(ham), whole(ham2), pl.BlockSpec((n, 2 * coupled), lambda k: (0, k))]
+        + [whole(a) for a in (src, u, g, hg)],
+        out_specs=whole(aux),
+        scratch_shapes=[pltpu.VMEM((rows, 2 * coupled), F32)] * 2,
+        compiler_params=pltpu.CompilerParams(vmem_limit_bytes=40 * 1024 * 1024),
+        cost_estimate=pl.CostEstimate(flops=4 * rows * n * 2 * coupled * modes, bytes_accessed=16 * 1024 * 1024, transcendentals=0),
+        name="modes",
+    )(lead, coef, aux, ham, ham2, pi, src, u, g, hg)
+
+
 def by_lead(x, gamma):
     leads, coupled = gamma.shape[:2]
     return jnp.concatenate(
@@ -334,39 +459,13 @@
     he_col = dot(ham_c, e_full).astype(BF)
     hg_col = by_lead(he_col, lead_gamma)
 
-    pi_b = auxiliary.astype(BF).reshape(rows, modes * 2 * coupled)
-
-    onehot = (lead_index[:, None] == jnp.arange(leads, dtype=jnp.int32)[None, :]).astype(F32)
-    lam_re, lam_im = -mode_width, mode_level
-    l_parts, m_parts = [[], []], [[], []]
-    for l in range(leads):
-        s = [sum(onehot[k, l] * auxiliary[:, k, p] for k in range(modes)) for p in range(2)]
-        m_re = sum(onehot[k, l] * (lam_re[k] * auxiliary[:, k, 0] - lam_im[k] * auxiliary[:, k, 1]) for k in range(modes))
-        m_im = sum(onehot[k, l] * (lam_re[k] * auxiliary[:, k, 1] + lam_im[k] * auxiliary[:, k, 0]) for k in range(modes))
-        for p in range(2):
-            l_parts[p].append(s[p])
-        m_parts[0].append(m_re)
-        m_parts[1].append(m_im)
-    l_part = jnp.concatenate(l_parts[0] + l_parts[1], axis=1)
-    m_part = jnp.concatenate(m_parts[0] + m_parts[1], axis=1)
-    w_l = jnp.concatenate([(residue[:, p][:, None] * onehot).sum(0) for p in range(2)])
-    v_l = jnp.concatenate([((residue[:, p] * occupation)[:, None] * onehot).sum(0) for p in range(2)])
-
     hrho_b = hrho_t.astype(BF)
     f_re = dot(jnp.concatenate([hrho_b[cols:], rho_t[cols:]], 0), jnp.concatenate([2 * g_col, -hg_col.astype(BF)], 0), 0, 0)
     f_im = dot(jnp.concatenate([hrho_b[:cols], rho_t[:cols]], 0), jnp.concatenate([-2 * g_col, hg_col.astype(BF)], 0), 0, 0)
-    f_part = jnp.concatenate([f_re, f_im], axis=1)
-    l_part_b = l_part.astype(BF)
-    n_part = jnp.concatenate([dot(l_part_b[:, :q], g_row, 0, 0), -dot(l_part_b[:, q:], g_row, 0, 0)], axis=1)
-
+    coef = jnp.stack([mode_level, mode_width, residue[:, 0], residue[:, 1], occupation])
+    aux = auxiliary.reshape(-1, coupled)
+    pi_b, payload = local_sums(lead_index, coef, aux, f_re, f_im, g_row)
     piece = rows // n_mode
-    n_piece = q // n_mode
-    scal = jnp.concatenate([w_l, v_l])
-    scal = jnp.zeros((n_mode, 4, 2 * q), F32).at[:, 0, : scal.shape[0]].set(scal)
-    payload = jnp.concatenate(
-        [a.reshape(n_mode, -1, 2 * q) for a in (l_part, m_part, f_part, n_part)] + [scal], axis=1
-    ).astype(BF)
-    payload = payload.reshape(NY, NZ, 2, 32, 2 * q).transpose(2, 0, 1, 3, 4)
     pi_all, panel, whole = exchange(pi_b, jnp.concatenate([rho_t, ham2_ct], 0), payload)
     pi_all = pi_all.reshape(n, -1)
     panel = panel.reshape(n_mode, 3, cols, rows)
@@ -376,8 +475,8 @@
     l1_b = whole[:, :piece].reshape(rows, 2 * q)
     m1 = whole[:, piece : 2 * piece].reshape(rows, 2 * q).astype(F32)
     f_all = whole[:, 2 * piece : 3 * piece].reshape(rows, 2 * q).astype(F32)
-    n_all = whole[:, 3 * piece : 3 * piece + n_piece].reshape(q, 2 * q)
-    scal = whole[0, 3 * piece + n_piece].astype(F32)
+    n_all = whole[0::2, 3 * piece :].reshape(q, 2 * q)
+    scal = whole[1, 3 * piece].astype(F32)
     w_sum, v_sum = scal[: 2 * leads], scal[2 * leads : 4 * leads]
 
     grow_full = by_lead(e_full, lead_gamma).astype(BF)
@@ -421,33 +520,11 @@
     out_im = -3.0 * comm[:cols] + base[cols:] + back_im - 2 * H2 * d_re
     density_rate = jnp.swapaxes(jnp.stack([out_re, out_im]), 1, 2)
 
-    h_pi = dot(hamiltonian, pi_all).reshape(rows, modes, 2, coupled)
-    h2_pi = dot(ham2_all, pi_all.reshape(n, -1), 0, 0).reshape(rows, modes, 2, coupled)
     lg = jnp.concatenate([by_lead(l1_b[:, p * q : (p + 1) * q], lead_gamma) for p in range(2)], 1)
     u = 2 * H2 * (f_all + lg + dot(e_row, n_all))
-    outs = []
-    for k in range(modes):
-        is0 = onehot[k, 0] > 0
-
-        def pick(a):
-            return jnp.where(is0, a[:, :coupled], a[:, coupled:])
-
-        lr, li = lam_re[k], lam_im[k]
-        wr, wi, occ = residue[k, 0], residue[k, 1], occupation[k]
-        sr, si, ur, ui = pick(s_re), pick(s_im), pick(u[:, :q]), pick(u[:, q:])
-        gk, hgk = pick(g_row_f), pick(hg_row)
-        br, bi = sr - occ * gk, si - occ * gk
-        ar, ai = 3 + 2 * H2 * lr, 2 * H2 * li
-        tr = ar * br - ai * bi + ur - 2 * H2 * occ * hgk
-        ti = ar * bi + ai * br + ui + 2 * H2 * occ * hgk
-        pr, pim = auxiliary[:, k, 0], auxiliary[:, k, 1]
-        cr = 3 * lr + 2 * H2 * (lr * lr - li * li)
-        ci = 3 * li + 4 * H2 * lr * li
-        er, ei = 4 * H2 * li, -3 - 4 * H2 * lr
-        hr, hi = h_pi[:, k, 0], h_pi[:, k, 1]
-        outs.append(cr * pr - ci * pim + er * hr - ei * hi - 2 * H2 * h2_pi[:, k, 0] + wr * tr - wi * ti)
-        outs.append(cr * pim + ci * pr + er * hi + ei * hr - 2 * H2 * h2_pi[:, k, 1] + wr * ti + wi * tr)
-    auxiliary_rate = jnp.stack(outs, axis=1).reshape(rows, modes, 2, coupled)
+    auxiliary_rate = advance_modes(
+        lead_index, coef, aux, hamiltonian, jnp.swapaxes(ham2_all, 0, 1), pi_all, src, u, g_row, hg_row
+    ).reshape(auxiliary.shape)
     return density_rate, auxiliary_rate
 
 

time: 319 us -> 152 us (0.48)
  other arithmetic: 80.2 us -> 3.34 us
  local copies, waits for them, and re-layouts: 69.7 us -> 16.6 us
  between operations: 32.2 us -> 1.44 us
  matrix products: 34.2 us -> 19 us
  Pallas kernels: 99.6 us -> 111 us
    another operation x8 -> x1, other arithmetic: 39.2 us -> 0.06 us
    concatenate x9 -> x0, local copies, waits for them, and re-layouts: 24.4 us -> none  [the longest x5 18.8 us: shards(): jnp.concatenate([a.reshape(n_mode, -1, 2 * q) for a in (l_part, m_part, f...]
    unnamed x8 -> x2, other arithmetic: 20.8 us -> 0.05 us
    unnamed x149 -> x80, local copies, waits for them, and re-layouts: 22.1 us -> 5.92 us
    dot_general x42 -> x38, matrix products: 34.2 us -> 19 us  [dot(): lax.dot_general(a, b, (((ca,), (cb,)), ((), ())), preferred_element_type=...]
    pallas_call x0 -> x2, Pallas kernels: none -> 11.5 us  [the longest x1 9.39 us: advance_modes(): pl.pallas_call(modes_kernel, grid=(modes,), out_shape=jax.ShapeDtypeStruc...]
    sub x3 -> x0, other arithmetic: 10.5 us -> none  [shards(): br, bi = (sr - occ * gk, si - occ * gk)]
    slice x10 -> x2, local copies, waits for them, and re-layouts: 7.4 us -> 0.63 us  [the longest x1 0.62 us: shards(): rho_t[:cols]]
where the time goes in v2:
time: 152 us; the launch traced here: 151 us
  Pallas kernels  111 us (73%)
  matrix products  19 us (12%)
  local copies, waits for them, and re-layouts  16.6 us (11%)
  other arithmetic  3.34 us (2%)
    pallas_call x1, Pallas kernels, exchange(): pl.pallas_call(main_kernel, out_shape=[jax.ShapeDtypeStruct((4, *pi.shape...  77.8 us
    pallas_call x2, Pallas kernels, over_row(): pl.pallas_call(rows_kernel, out_shape=jax.ShapeDtypeStruct((blk.shape[0],...  21.6 us
    dot_general x38, matrix products, dot(): lax.dot_general(a, b, (((ca,), (cb,)), ((), ())), preferred_element_type=...  19 us
    pallas_call x1, Pallas kernels, advance_modes(): pl.pallas_call(modes_kernel, grid=(modes,), out_shape=jax.ShapeDtypeStruc...  9.39 us
    unnamed x80, local copies, waits for them, and re-layouts  5.92 us
    slice x1, local copies, waits for them, and re-layouts, shards(): ham2_all = panel[:, 2].reshape(n, rows)  5.61 us
    another operation x1, local copies, waits for them, and re-layouts, shards(): ham2_all = panel[:, 2].reshape(n, rows)  3.96 us

profile of v2, /device:TPU:1, one launch (start us, length us, event | category | flops | bytes accessed | tf_op | source)
XLA Modules:
  0.0 151.4 jit_solution(1849839797445160337)
XLA Ops:
  0.7 3.2 %convolution_convert_fusion.2 = bf16[256,512]{1,0:T(8,128)(2,1)} fusion(bf16[512,2048]{1,0:T(8,128)(2,1)} %ham.1, s32[256]{0:T(256)} %bitcast.135), kind=kOutput, calls=%fused_computation.5 | convolution fusion | flops 538050560 | bytes 2360320 | tf_op jit(solution)/shard_map/dot_general | solution.py:14
  4.0 0.6 slice_bitcast_fusion.3
  4.9 0.4 copy-done.20
  5.3 9.1 %rows.2 = bf16[96,2048]{1,0:T(8,128)(2,1)S(1)} custom-call(bf16[96,512]{1,0:T(8,128)(2,1)S(1)} %pad_maximum_fusion.7.blk), custom_call_target="tpu_custom_call" | custom-call | tf_op jit(solution)/shard_map/rows/pallas_call | solution.py:287
  14.4 0.8 fusion.154
  15.4 0.4 copy-done.32
  15.9 0.5 convolution_convert_fusion.6
  17.7 0.9 convolution_convert_fusion.3
  18.7 1.0 convolution_convert_fusion.4
  19.8 1.6 %copy-done.3 = f32[512,4,2,128]{3,2,1,0:T(2,128)S(1)} copy-done((f32[512,4,2,128]{3,2,1,0:T(2,128)S(1)}, f32[512,4,2,128]{3,2,1,0:T(2,128)}, u32[]{:S(2)}) %copy-start.3) | copy-done | bytes 2097176
  21.4 2.1 %sums.1 = (bf16[512,1024]{1,0:T(8,128)(2,1)S(1)}, bf16[2,4,8,32,512]{4,3,2,1,0:T(8,128)(2,1)S(1)}) custom-call(s32[4]{0:T(128)S(1)} %copy-done.8, f32[5,4]{1,0:T(8,128)S(1)} %stack.24.coef, f32[4096,128]{1,0:T(8,128)S(1)} %bitcast.118, f32[512,256]{1,0:T(8,128)S(1)} %fusion.65.f_re, f32[512,256]{1,0:T(8,128)S(1)} %fusion.69.f_im, ...), custom_call_target="tpu_custom_call" | custom-call | tf_op jit(solution)/shard_map/sums/pallas_call | solution.py:351
  23.6 77.8 %exchange.1 = (bf16[4,512,1024]{2,1,0:T(8,128)(2,1)}, bf16[4,8,2,96,512]{4,3,2,1,0:T(8,128)(2,1)}, bf16[4,8,2,32,512]{4,3,2,1,0:T(8,128)(2,1)S(1)}) custom-call(bf16[512,1024]{1,0:T(8,128)(2,1)S(1)} %get-tuple-element.7.pi, bf16[96,512]{1,0:T(8,128)(2,1)S(1)} %pad_maximum_fusion.8.blk, bf16[2,4,8,32,512]{4,3,2,1,0:T(8,128)(2,1)S(1)} %get-tuple-element.8.pay), custom_call_target="tpu_custom_call" | custom-call | tf_op jit(solution)/shard_map/exchange/pallas_call | solution.py:243
  101.9 5.6 %fusion.152 = (bf16[64,1,32,512]{3,2,1,0:T(8,128)(2,1)}, bf16[64,1,32,512]{3,2,1,0:T(8,128)(2,1)S(1)}, bf16[64,1,32,512]{3,2,1,0:T(8,128)(2,1)S(1)}) fusion(bf16[64,3,32,512]{3,2,1,0:T(8,128)(2,1)} %bitcast.129), kind=kLoop, calls=%fused_computation.222 | loop fusion | bytes 12582912 | tf_op jit(solution)/shard_map/slice | solution.py:472
  107.5 0.5 fusion.146
  107.9 0.5 fusion.148
  108.4 0.4 copy-done.10
  108.8 0.7 copy-done.12
  109.6 1.2 fusion.9
  111.9 0.5 copy-done.11
  112.4 0.8 fusion.20
  113.2 0.8 copy-done.2
  114.7 1.6 %fusion.21 = (f32[512,256]{1,0:T(8,128)S(1)}, f32[512,256]{1,0:T(8,128)S(1)}, f32[512,256]{1,0:T(8,128)}) fusion(f32[512,256]{1,0:T(8,128)S(1)} %fusion.20, f32[256]{0:T(256)S(1)} %broadcast_bitcast_fusion.1, f32[256]{0:T(256)S(1)} %broadcast_bitcast_fusion.2, f32[256]{0:T(256)S(1)} %broadcast_bitcast_fusion.3, bf16[512,128]{1,0:T(8,128)(2,1)S(1)} %copy-done.28, ...), kind=kOutput, calls=%fused_computation.46 | convolution fusion | flops 540803072 | bytes 5509120 | tf_op jit(solution)/shard_map/dot_general | solution.py:14
  116.6 12.6 %rows.3 = bf16[192,2048]{1,0:T(8,128)(2,1)S(1)} custom-call(bf16[192,512]{1,0:T(8,128)(2,1)S(1)} %multiply_dynamic-update-slice_fusion.blk), custom_call_target="tpu_custom_call" | custom-call | tf_op jit(solution)/shard_map/rows/pallas_call | solution.py:287
  129.6 0.5 fusion.60
  130.1 0.5 fusion.62
  130.9 0.8 fusion.2
  132.7 0.7 maximum_bitcast_fusion
  133.3 4.0 %copy.36 = bf16[2048,512]{0,1:T(8,128)(2,1)} copy(bf16[2048,512]{1,0:T(8,128)(2,1)} %bitcast.128) | data formatting | bytes 4194304 | tf_op jit(solution)/shard_map/reshape;squeeze | solution.py:472
  137.3 1.5 pad_maximum_fusion.1.src
  139.5 1.6 %fusion.u = f32[512,512]{1,0:T(8,128)S(1)} fusion(f32[512,128]{1,0:T(8,128)S(1)} %fusion.50, f32[512,128]{1,0:T(8,128)S(1)} %fusion.52, f32[512,128]{1,0:T(8,128)S(1)} %fusion.54, f32[512,128]{1,0:T(8,128)S(1)} %fusion.56, bf16[64,32,512]{2,1,0:T(8,128)(2,1)} %bitcast.115, s32[256]{0:T(256)S(1)} %bitcast.146, s32[512]{0:T(512)S(1)} %iota_add_fusion), kind=kOutput, calls=%fused_computation.4 | convolution fusion | flops 136183808 | bytes 2886656 | tf_op jit(solution)/shard_map/dot_general | solution.py:14
  141.6 0.4 copy-done.5
  142.0 9.4 %modes.1 = f32[4096,128]{1,0:T(8,128)} custom-call(s32[4]{0:T(128)S(1)} %copy-done.8, f32[5,4]{1,0:T(8,128)S(1)} %stack.24.coef, f32[4096,128]{1,0:T(8,128)S(1)} %bitcast.119, bf16[512,2048]{1,0:T(8,128)(2,1)S(1)} %copy-done, bf16[512,2048]{1,0:T(8,128)(2,1)S(1)} %bitcast.120, bf16[2048,1024]{1,0:T(8,128)(2,1)S(1)} %bitcast.121, ...), custom_call_target="tpu_custom_call" | custom-call | flops 4294967296 | bytes 16777216 | tf_op jit(solution)/shard_map/modes/pallas_call | solution.py:410
  (129 shorter events, 7.3 us)
Async XLA Ops:
  0.6 3.3 %copy-start.36 = (f32[4]{0:T(128)S(1)}, f32[4]{0:T(128)}, u32[]{:S(2)}) copy-start(f32[4]{0:T(128)} %param.15) | copy-start | bytes 52
  0.6 3.3 %copy-start.37 = (f32[4]{0:T(128)S(1)}, f32[4]{0:T(128)}, u32[]{:S(2)}) copy-start(f32[4]{0:T(128)} %param.16) | copy-start | bytes 52
  0.7 3.3 %copy-start.35 = (f32[4,2]{0,1:T(2,128)S(1)}, f32[4,2]{0,1:T(2,128)}, u32[]{:S(2)}) copy-start(f32[4,2]{0,1:T(2,128)} %param.17) | copy-start | bytes 100
  0.7 3.3 %copy-start.38 = (f32[4]{0:T(128)S(1)}, f32[4]{0:T(128)}, u32[]{:S(2)}) copy-start(f32[4]{0:T(128)} %param.18) | copy-start | bytes 52
  0.7 3.3 %copy-start.22 = (f32[2,512,32]{1,2,0:T(8,128)S(1)}, f32[2,512,32]{1,2,0:T(8,128)}, u32[]{:S(2)}) copy-start(f32[2,512,32]{1,2,0:T(8,128)} %param.10) | copy-start | bytes 393220
  0.7 4.0 %copy-start = (bf16[512,2048]{1,0:T(8,128)(2,1)S(1)}, bf16[512,2048]{1,0:T(8,128)(2,1)}, u32[]{:S(2)}) copy-start(bf16[512,2048]{1,0:T(8,128)(2,1)} %ham.1) | copy-start | bytes 6291460
  4.6 10.6 %copy-start.31 = (s32[2,128]{1,0:T(2,128)S(1)}, s32[2,128]{1,0:T(2,128)}, u32[]{:S(2)}) copy-start(s32[2,128]{1,0:T(2,128)} %param.13) | copy-start | bytes 3076
  4.6 10.7 %copy-start.18 = (bf16[2,128,128]{2,1,0:T(8,128)(2,1)S(1)}, bf16[2,128,128]{2,1,0:T(8,128)(2,1)}, u32[]{:S(2)}) copy-start(bf16[2,128,128]{2,1,0:T(8,128)(2,1)} %param.19) | copy-start | bytes 196612
  14.3 2.9 %copy-start.26 = (bf16[32,512]{1,0:T(8,128)(2,1)S(1)}, bf16[32,512]{1,0:T(8,128)(2,1)}, u32[]{:S(2)}) copy-start(bf16[32,512]{1,0:T(8,128)(2,1)} %get-tuple-element.21) | copy-start | bytes 98308
  15.2 4.6 %copy-start.8 = (s32[4]{0:T(128)S(1)}, s32[4]{0:T(128)}, u32[]{:S(2)}) copy-start(s32[4]{0:T(128)} %lead.3) | copy-start | bytes 52
  18.6 4.9 %copy-start.27 = (bf16[512,128]{1,0:T(8,128)(2,1)}, bf16[512,128]{1,0:T(8,128)(2,1)S(1)}, u32[]{:S(2)}) copy-start(bf16[512,128]{1,0:T(8,128)(2,1)S(1)} %convolution_convert_fusion.3) | copy-start | bytes 393220
  18.6 4.9 %copy-start.16 = (f32[96,512]{1,0:T(8,128)S(1)}, f32[96,512]{1,0:T(8,128)}, u32[]{:S(2)}) copy-start(f32[96,512]{1,0:T(8,128)} %copy-done.15) | copy-start | bytes 589828
  18.7 4.9 %copy-start.21 = (bf16[2,512,32]{1,2,0:T(8,128)(2,1)S(1)}, bf16[2,512,32]{1,2,0:T(8,128)(2,1)}, u32[]{:S(2)}) copy-start(bf16[2,512,32]{1,2,0:T(8,128)(2,1)} %copy-done.20) | copy-start | bytes 196612
  19.7 3.9 %copy-start.29 = (bf16[512,128]{1,0:T(8,128)(2,1)}, bf16[512,128]{1,0:T(8,128)(2,1)S(1)}, u32[]{:S(2)}) copy-start(bf16[512,128]{1,0:T(8,128)(2,1)S(1)} %convolution_convert_fusion.4) | copy-start | bytes 393220
  19.8 1.6 %copy-start.3 = (f32[512,4,2,128]{3,2,1,0:T(2,128)S(1)}, f32[512,4,2,128]{3,2,1,0:T(2,128)}, u32[]{:S(2)}) copy-start(f32[512,4,2,128]{3,2,1,0:T(2,128)} %param.11) | copy-start | bytes 6291460
  21.4 2.2 %copy-start.6 = (bf16[512,256]{1,0:T(8,128)(2,1)}, bf16[512,256]{1,0:T(8,128)(2,1)S(1)}, u32[]{:S(2)}) copy-start(bf16[512,256]{1,0:T(8,128)(2,1)S(1)} %pad_maximum_fusion.5.g_row.g) | copy-start | bytes 786436
  23.6 77.9 %copy-start.33 = (s32[32]{0:T(128)S(1)}, s32[32]{0:T(128)}, u32[]{:S(2)}) copy-start(s32[32]{0:T(128)} %copy-done.32) | copy-start | bytes 388
  101.4 6.1 %copy-start.1 = (bf16[4,8,2,32,512]{4,3,2,1,0:T(8,128)(2,1)}, bf16[4,8,2,32,512]{4,3,2,1,0:T(8,128)(2,1)S(1)}, u32[]{:S(2)}) copy-start(bf16[4,8,2,32,512]{4,3,2,1,0:T(8,128)(2,1)S(1)} %get-tuple-element.10) | copy-start | bytes 6291460
  107.5 2.0 %copy-start.12 = (bf16[64,1,32,512]{3,2,1,0:T(8,128)(2,1)}, bf16[64,1,32,512]{3,2,1,0:T(8,128)(2,1)S(1)}, u32[]{:S(2)}) copy-start(bf16[64,1,32,512]{3,2,1,0:T(8,128)(2,1)S(1)} %get-tuple-element.15) | copy-start | bytes 6291460
  107.9 3.3 %copy-start.19 = (bf16[2,128,128]{2,1,0:T(8,128)(2,1)S(1)}, bf16[2,128,128]{2,1,0:T(8,128)(2,1)}, u32[]{:S(2)}) copy-start(bf16[2,128,128]{2,1,0:T(8,128)(2,1)} %param.19) | copy-start | bytes 196612
  110.8 1.6 %copy-start.11 = (bf16[64,1,32,512]{3,2,1,0:T(8,128)(2,1)S(1)}, bf16[64,1,32,512]{3,2,1,0:T(8,128)(2,1)}, u32[]{:S(2)}) copy-start(bf16[64,1,32,512]{3,2,1,0:T(8,128)(2,1)} %copy-done.10) | copy-start | bytes 6291460
  112.4 1.6 %copy-start.2 = (bf16[4,8,2,32,512]{4,3,2,1,0:T(8,128)(2,1)S(1)}, bf16[4,8,2,32,512]{4,3,2,1,0:T(8,128)(2,1)}, u32[]{:S(2)}) copy-start(bf16[4,8,2,32,512]{4,3,2,1,0:T(8,128)(2,1)} %copy-done.1) | copy-start | bytes 6291460
  112.4 2.2 %copy-start.13 = (bf16[64,1,32,512]{3,2,1,0:T(8,128)(2,1)S(1)}, bf16[64,1,32,512]{3,2,1,0:T(8,128)(2,1)}, u32[]{:S(2)}) copy-start(bf16[64,1,32,512]{3,2,1,0:T(8,128)(2,1)} %copy-done.12) | copy-start | bytes 6291460
  112.4 2.2 %copy-start.28 = (bf16[512,128]{1,0:T(8,128)(2,1)S(1)}, bf16[512,128]{1,0:T(8,128)(2,1)}, u32[]{:S(2)}) copy-start(bf16[512,128]{1,0:T(8,128)(2,1)} %copy-done.27) | copy-start | bytes 393220
  112.4 2.2 %copy-start.30 = (bf16[512,128]{1,0:T(8,128)(2,1)S(1)}, bf16[512,128]{1,0:T(8,128)(2,1)}, u32[]{:S(2)}) copy-start(bf16[512,128]{1,0:T(8,128)(2,1)} %copy-done.29) | copy-start | bytes 393220
  114.0 15.4 %copy-start.23 = (f32[512,256]{1,0:T(8,128)}, f32[512,256]{1,0:T(8,128)S(1)}, u32[]{:S(2)}) copy-start(f32[512,256]{1,0:T(8,128)S(1)} %fusion.20) | copy-start | bytes 1572868
  116.5 12.8 %copy-start.14 = (bf16[256,512]{1,0:T(8,128)(2,1)S(1)}, bf16[256,512]{1,0:T(8,128)(2,1)}, u32[]{:S(2)}) copy-start(bf16[256,512]{1,0:T(8,128)(2,1)} %convolution_convert_fusion.2) | copy-start | bytes 786436
  116.5 12.9 %copy-start.25 = (bf16[32,256]{1,0:T(8,128)(2,1)S(1)}, bf16[32,256]{1,0:T(8,128)(2,1)}, u32[]{:S(2)}) copy-start(bf16[32,256]{1,0:T(8,128)(2,1)} %copy-done.24) | copy-start | bytes 49156
  137.3 4.3 %copy-start.9 = (bf16[4,512,1024]{2,1,0:T(8,128)(2,1)S(1)}, bf16[4,512,1024]{2,1,0:T(8,128)(2,1)}, u32[]{:S(2)}) copy-start(bf16[4,512,1024]{2,1,0:T(8,128)(2,1)} %get-tuple-element.11) | copy-start | bytes 12582916
  139.4 2.2 %copy-start.4 = (f32[512,4,2,128]{3,2,1,0:T(2,128)S(1)}, f32[512,4,2,128]{3,2,1,0:T(2,128)}, u32[]{:S(2)}) copy-start(f32[512,4,2,128]{3,2,1,0:T(2,128)} %param.11) | copy-start | bytes 6291460
  139.5 2.5 %copy-start.5 = (bf16[2048,512]{0,1:T(8,128)(2,1)S(1)}, bf16[2048,512]{0,1:T(8,128)(2,1)}, u32[]{:S(2)}) copy-start(bf16[2048,512]{0,1:T(8,128)(2,1)} %copy.36) | copy-start | bytes 6291460
  139.5 2.5 %copy-start.7 = (bf16[512,256]{1,0:T(8,128)(2,1)S(1)}, bf16[512,256]{1,0:T(8,128)(2,1)}, u32[]{:S(2)}) copy-start(bf16[512,256]{1,0:T(8,128)(2,1)} %copy-done.6) | copy-start | bytes 786436
  (7 other events, 6.8 us)

commit v3 on v2

v3 whole, which is shorter than its diff:
```python
import jax
import jax.numpy as jnp
from jax import lax
from jax.experimental import pallas as pl
from jax.experimental.pallas import tpu as pltpu
from jax.sharding import PartitionSpec as P

H2 = 0.05
F32 = jnp.float32
BF = jnp.bfloat16


def dot(a, b, ca=1, cb=0):
    return lax.dot_general(a, b, (((ca,), (cb,)), ((), ())), preferred_element_type=F32)


MESH = pl.DeviceIdType.MESH
NY, NZ = 4, 8


class Net:
    def __init__(self, send, recv):
        self.send, self.recv, self.used, self.sent = send, recv, 0, []
        m = lax.axis_index("mode")
        self.x = lax.axis_index("row")
        self.c, self.z, self.y = lax.rem(m, 2), lax.rem(m // 2, NZ), m // (2 * NZ)

    def dev(self, y=None, z=None, c=None, x=None):
        y = self.y if y is None else y
        z = self.z if z is None else z
        c = self.c if c is None else c
        return {"mode": (y * NZ + z) * 2 + c, "row": self.x if x is None else x}

    def at(self, name, d):
        size = {"x": 4, "y": NY, "z": NZ}[name]
        return lax.rem(getattr(self, name) + (d % size), size)

    def slot(self):
        self.used += 1
        return self.used - 1

    def start(self, src, dst, to, slot):
        copy = pltpu.make_async_remote_copy(
            src_ref=src, dst_ref=dst, send_sem=self.send.at[slot], recv_sem=self.recv.at[slot], device_id=to, device_id_type=MESH
        )
        copy.start()
        self.sent.append(copy)

    def arrive(self, ref, slot):
        pltpu.make_async_remote_copy(
            src_ref=ref, dst_ref=ref, send_sem=self.send.at[slot], recv_sem=self.recv.at[slot],
            device_id=self.dev(c=1 - self.c), device_id_type=MESH,
        ).wait_recv()

    def finish(self):
        for copy in self.sent:
            copy.wait_send()

    def greet(self, peers):
        barrier = pltpu.get_barrier_semaphore()
        for peer in peers:
            pl.semaphore_signal(barrier, inc=1, device_id=peer, device_id_type=MESH)
        pl.semaphore_wait(barrier, len(peers))


def ring(net, name, part, share, t, step):
    size = {"x": 4, "y": NY, "z": NZ}[name]
    far = size // 2
    slots = {(d, s): net.slot() for s in range(1, far + 1) for d in (1, -1)}
    at = lambda d: net.at(name, d)
    for d in (1, -1):
        net.start(part(at(0), None), part(at(0), None), net.dev(**{name: at(d)}), slots[d, 1])
    share(at(0))
    for s in range(1, far + 1):
        yield t + s * step
        for d in (1, -1):
            half = None if s < far else (d + 1) // 2
            net.arrive(part(at(-d * s), half), slots[d, s])
            if s < far:
                half = None if s + 1 < far else (d + 1) // 2
                net.start(part(at(-d * s), half), part(at(-d * s), half), net.dev(**{name: at(d)}), slots[d, s + 1])
        if s < far:
            share(at(s))
            share(at(-s))
        else:
            share(at(far))


def gather_plane(net, buf, t, unit):
    rows, lanes = buf.shape[-2:]
    lane = {None: pl.ds(0, lanes), 0: pl.ds(0, lanes // 2), 1: pl.ds(lanes // 2, lanes // 2)}
    low, high = pl.ds(0, rows // 2), pl.ds(rows // 2, rows // 2)
    c = net.c
    waits = []

    def share_of(ref_of):
        def share(pos):
            slot = net.slot()
            mine, theirs = ref_of(pos, c), ref_of(pos, 1 - c)
            net.start(mine, mine, net.dev(c=1 - c), slot)
            waits.append((theirs, slot))
        return share

    def nothing(pos):
        pass

    def first():
        yield from ring(net, "y", lambda p, h: buf.at[:, p, net.z, c, low, lane[h]], nothing, t, 2.0 + unit)
        yield from ring(
            net, "z", lambda p, h: buf.at[:, :, p, c, low, lane[h]],
            share_of(lambda p, cc: buf.at[:, :, p, cc, low, lane[None]]), t + 5.0 + 2 * unit, 2.0 + 4 * unit,
        )

    def second():
        yield from ring(net, "z", lambda p, h: buf.at[:, net.y, p, c, high, lane[h]], nothing, t, 2.0 + unit)
        yield from ring(
            net, "y", lambda p, h: buf.at[:, p, :, c, high, lane[h]],
            share_of(lambda p, cc: buf.at[:, p, :, cc, high, lane[None]]), t + 9.0 + 4 * unit, 2.0 + 8 * unit,
        )

    yield from merge([first(), second()])
    yield t + 12.0 + 30 * unit
    for ref, slot in waits:
        net.arrive(ref, slot)


def gather_small(net, whole, rows, lanes, t, unit):
    c = net.c
    slots = [net.slot() for _ in range(NZ - 1)]
    mine = whole.at[net.y, net.z, c, rows, lanes]
    for d in (4, 3, 5, 2, 6, 1, 7):
        net.start(mine, mine, net.dev(z=net.at("z", d)), slots[d - 1])
    yield t + 4.0 + 10 * unit
    for d in (1, 7, 2, 6, 3, 5, 4):
        net.arrive(whole.at[net.y, net.at("z", -d), c, rows, lanes], slots[d - 1])
    cuts = {None: pl.ds(0, NZ), 0: pl.ds(0, NZ // 2), 1: pl.ds(NZ // 2, NZ // 2)}
    waits = []

    def share(pos):
        slot = net.slot()
        ref = whole.at[pos, :, c, rows, lanes]
        net.start(ref, ref, net.dev(c=1 - c), slot)
        waits.append((whole.at[pos, :, 1 - c, rows, lanes], slot))

    yield from ring(net, "y", lambda p, h: whole.at[p, cuts[h], c, rows, lanes], share, t + 4.0 + 10 * unit, 2.0 + 6 * unit)
    yield t + 10.0 + 24 * unit
    for ref, slot in waits:
        net.arrive(ref, slot)


def merge(threads):
    live = []
    for thread in threads:
        when = next(thread, None)
        if when is not None:
            live.append([when, len(live), thread])
    while live:
        live.sort(key=lambda item: (item[0], item[1]))
        yield live[0][0]
        when = next(live[0][2], None)
        if when is None:
            live.pop(0)
        else:
            live[0][0] = when


def reduce_plane(net, chain, pay, whole, tails, scal, xs, pair, acc, got1, got2, gotz, t):
    c, y, z = net.c, net.y, net.z
    width = got2.shape[-1]
    ln = pl.ds(chain * width, width)
    slot = net.slot()
    net.start(pay.at[1 - c, :, :, :, ln], pair.at[:, :, :, ln], net.dev(c=1 - c), slot)
    yield t + 2.0
    net.arrive(pair.at[:, :, :, ln], slot)

    def add_pair(i, carry):
        acc[i, :, :, ln] = (pay[c, i, :, :, ln].astype(F32) + pair[i, :, :, ln].astype(F32)).astype(BF)
        return carry

    lax.fori_loop(0, NY, add_pair, 0)
    near, over = y + 1 - 2 * lax.rem(y, 2), NY - 1 - y
    half = NZ // 2
    colors = []
    for color, (f, s) in enumerate(((near, over), (over, near))):
        s_of_f = lax.rem(y + 2, NY)
        zs = pl.ds(color * half, half)
        slots = [net.slot() for _ in range(3)]
        net.start(acc.at[s_of_f, zs, :, ln], got1.at[chain, color, 1], net.dev(y=f), slots[1])
        net.start(acc.at[f, zs, :, ln], got1.at[chain, color, 0], net.dev(y=f), slots[0])
        colors.append((f, s, zs, slots))
    yield t + 5.5
    for color, (f, s, zs, slots) in enumerate(colors):
        net.arrive(got1.at[chain, color, 1], slots[1])
        acc[s, zs, :, ln] = (acc[s, zs, :, ln].astype(F32) + got1[chain, color, 1].astype(F32)).astype(BF)
        net.start(acc.at[s, zs, :, ln], got2.at[chain, color], net.dev(y=s), slots[2])
    yield t + 9.5
    for color, (f, s, zs, slots) in enumerate(colors):
        net.arrive(got1.at[chain, color, 0], slots[0])
        net.arrive(got2.at[chain, color], slots[2])
        total = acc[y, zs, :, ln].astype(F32) + got1[chain, color, 0].astype(F32) + got2[chain, color].astype(F32)
        acc[y, zs, :, ln] = total.astype(BF)
    zslots = [net.slot() for _ in range(NZ - 1)]
    for d in (4, 3, 5, 2, 6, 1, 7):
        net.start(acc.at[y, net.at("z", d), :, ln], gotz.at[chain, d - 1], net.dev(z=net.at("z", d)), zslots[d - 1])
    yield t + 16.0
    total = acc[y, z, :, ln].astype(F32)
    for d in range(1, NZ):
        net.arrive(gotz.at[chain, d - 1], zslots[d - 1])
        total = total + gotz[chain, d - 1].astype(F32)
    whole[y, z, c, :, ln] = total[:16].astype(BF)
    tails[pl.ds(0, 8), ln] = total[16:24]
    xs[0, :, ln] = total[24:]
    slots = [net.slot() for _ in range(4)]
    mine = xs.at[0, :, ln]
    net.start(mine, xs.at[4, :, ln], net.dev(c=1 - c), slots[0])
    for d in (1, 2, 3):
        net.start(mine, xs.at[d, :, ln], net.dev(x=net.at("x", d)), slots[d])

    def small_ends():
        yield t + 34.0
        for d, slot in zip((4, 1, 2, 3), slots):
            net.arrive(xs.at[d, :, ln], slot)
        tails[pl.ds(8, 8), ln] = xs[0, :, ln] + xs[1, :, ln] + xs[2, :, ln] + xs[3, :, ln]
        scal[:, ln] = jnp.where(jnp.full((8, width), c) == 1, xs[0, :, ln], xs[4, :, ln])

    yield from merge([gather_small(net, whole, pl.ds(0, 16), ln, t + 16.0, 0.2), small_ends()])


def gather_rows(net, pall):
    rows = pall.shape[1] // 2
    halves = (pl.ds(0, rows), pl.ds(rows, rows))
    x = net.x
    slots = {(d, i): net.slot() for d in (0, 1) for i in range(3)}
    for i in (0, 1):
        for d, way in ((0, 1), (1, -1)):
            ref = pall.at[x, halves[i if d == 0 else 1 - i]]
            net.start(ref, ref, net.dev(x=net.at("x", way)), slots[d, i])
    yield 16.0
    for d, way in ((0, 1), (1, -1)):
        ref = pall.at[net.at("x", -way), halves[d]]
        net.arrive(ref, slots[d, 0])
        net.start(ref, ref, net.dev(x=net.at("x", way)), slots[d, 2])
    yield 40.0
    for d, way in ((0, 1), (1, -1)):
        net.arrive(pall.at[net.at("x", -way), halves[1 - d]], slots[d, 1])
        net.arrive(pall.at[net.at("x", -2), halves[d]], slots[d, 2])


def spread_rows(net, src, place):
    slots = [net.slot() for _ in range(3)]
    for d in (2, 1, 3):
        net.start(src, place(net.x), net.dev(x=net.at("x", d)), slots[d - 1])

    def arrived():
        for d in (1, 3, 2):
            net.arrive(place(net.at("x", -d)), slots[d - 1])

    return arrived


def lanes_of(ref, x, lanes):
    at = pl.ds(pl.multiple_of(x * lanes, lanes), lanes)
    return ref.at[(slice(None),) * (len(ref.shape) - 1) + (at,)]


def front_kernel(
    lead, coef, aux, blk, ham, flat, gamma,
    first, hrho, ham2x, pall, panel, ham2, whole, tails, scal, grow, he_row, hg_row, he_col,
    picks, xs, own2, pay, held, pair, acc, got1, got2, gotz, send, recv,
):
    net = Net(send, recv)
    c, y, z, x = net.c, net.y, net.z, net.x
    peers = [net.dev(x=net.at("x", d)) for d in (1, 2, 3)]
    peers += [net.dev(y=net.at("y", d)) for d in (1, 3)]
    peers += [net.dev(z=net.at("z", d)) for d in range(1, NZ)]
    peers += [net.dev(c=1 - c)]
    net.greet(peers)
    cols, rows = blk.shape[1:]
    arrived = spread_rows(net, blk, lambda at: lanes_of(first, at, rows))
    panel[:, y, z, c] = blk[1:]
    lanes_of(first, x, rows)[...] = blk[...]

    def pick(i, carry):
        at = pl.ds(pl.multiple_of(256 * i, 256), 256)
        here = 256 * i + lax.broadcasted_iota(jnp.int32, (256, flat.shape[1]), 0)
        e = jnp.where(here == flat[...], 1.0, 0.0).astype(BF)
        picks[at, :] = e
        grow[at, :] = by_lead(e, gamma).astype(BF)
        return carry

    def work():
        lax.fori_loop(0, picks.shape[0] // 256, pick, 0)
        g_row = grow[pl.ds(pl.multiple_of(x * rows, rows), rows), :]
        sums(lead, coef, aux, g_row, pall, x, pay, held)
        rows_thread = gather_rows(net, pall)
        start = next(rows_thread)
        yield from merge([more(), resumed(rows_thread, start)])

    def more():
        yield 9.0
        arrived()
        applied = dot(first[...].reshape(3 * cols, -1), ham[...], 1, 1)
        own2[...] = applied[:cols].astype(BF)
        ham2[0, y, z, c] = own2[...]
        hrho[...] = applied[cols:]
        hg = dot(first[0], grow[...]).astype(BF)
        lhs = jnp.concatenate([applied[cols:].astype(BF), blk[1:].reshape(2 * cols, rows)], axis=0)
        me = (y * NZ + z) * 2 + c
        g2 = 2 * grow[pl.ds(pl.multiple_of(me * cols, cols), cols), :]
        for i, (sign, p) in enumerate(((1, 1), (-1, 0))):
            left = jnp.concatenate([lhs[p * cols : (p + 1) * cols], lhs[(2 + p) * cols : (3 + p) * cols]], axis=0)
            f = dot(left, sign * jnp.concatenate([g2, -hg], axis=0), 0, 0)
            q = f.shape[1]
            f = f.astype(BF).reshape(NY, NZ, 2, 8, q)
            for cc in range(2):
                pay[cc, :, :, 16:24, i * q : (i + 1) * q] = f[:, :, cc]
        chains = [reduce_plane(net, i, pay, whole, tails, scal, xs, pair, acc, got1, got2, gotz, 10.0 + 3.0 * i) for i in range(2)]
        spread = spread_ham2()
        yield from merge([*chains, gather_plane(net, ham2, 11.0, 0.4), spread, spare()])

    def spare():
        yield 13.8
        he_row[...] = dot(ham[...], picks[...]).astype(BF)
        hg_row[...] = dot(ham[...], grow[...])
        he_col[...] = dot(first[0], picks[...]).astype(BF)

    def spread_ham2():
        here = spread_rows(net, own2, lambda at: lanes_of(ham2x, at, rows))
        lanes_of(ham2x, x, rows)[...] = own2[...]
        yield 41.0
        here()

    for _ in merge([gather_plane(net, panel, 1.0, 0.75), work()]):
        pass
    net.finish()


def resumed(thread, start):
    yield start
    yield from thread


def front(lead, coef, aux, blk, ham, flat, gamma):
    cols, lanes = blk.shape[1:]
    half = lanes // 2
    n = ham.shape[1]
    vm = pl.BlockSpec(memory_space=pltpu.VMEM)
    sm = pl.BlockSpec(memory_space=pltpu.SMEM)
    sems = 192
    return pl.pallas_call(
        front_kernel,
        out_shape=[
            jax.ShapeDtypeStruct((3, cols, n), BF),
            jax.ShapeDtypeStruct((2 * cols, lanes), F32),
            jax.ShapeDtypeStruct((cols, n), BF),
            jax.ShapeDtypeStruct((4, lanes, aux.size // lanes), BF),
            jax.ShapeDtypeStruct((2, NY, NZ, 2, cols, lanes), BF),
            jax.ShapeDtypeStruct((1, NY, NZ, 2, cols, lanes), BF),
            jax.ShapeDtypeStruct((NY, NZ, 2, 16, lanes), BF),
            jax.ShapeDtypeStruct((16, lanes), F32),
            jax.ShapeDtypeStruct((8, lanes), F32),
            jax.ShapeDtypeStruct((n, flat.shape[1]), BF),
            jax.ShapeDtypeStruct((lanes, flat.shape[1]), BF),
            jax.ShapeDtypeStruct((lanes, flat.shape[1]), F32),
            jax.ShapeDtypeStruct((cols, flat.shape[1]), BF),
        ],
        in_specs=[sm, sm] + [vm] * 5,
        out_specs=[vm] * 13,
        scratch_shapes=[
            pltpu.VMEM((n, flat.shape[1]), BF),
            pltpu.VMEM((5, 8, lanes), F32),
            pltpu.VMEM((cols, lanes), BF),
            pltpu.VMEM((2, NY, NZ, 32, lanes), BF),
            pltpu.VMEM((lanes, lanes), BF),
            pltpu.VMEM((NY, NZ, 32, lanes), BF),
            pltpu.VMEM((NY, NZ, 32, lanes), BF),
            pltpu.VMEM((2, 2, 2, NZ // 2, 32, half), BF),
            pltpu.VMEM((2, 2, NZ // 2, 32, half), BF),
            pltpu.VMEM((2, NZ - 1, 32, half), BF),
            pltpu.SemaphoreType.DMA((sems,)),
            pltpu.SemaphoreType.DMA((sems,)),
        ],
        compiler_params=pltpu.CompilerParams(collective_id=1, has_side_effects=True, vmem_limit_bytes=30 * 1024 * 1024),
        cost_estimate=pl.CostEstimate(flops=10**11, bytes_accessed=2**24, transcendentals=0),
        name="front",
    )(lead, coef, aux, blk, ham, flat, gamma)


def back_kernel(blk, tails, out, n_all, send, recv):
    net = Net(send, recv)
    peers = [net.dev(x=net.at("x", d)) for d in (1, 2, 3)]
    peers += [net.dev(y=net.at("y", d)) for d in (1, 3)]
    peers += [net.dev(z=net.at("z", d)) for d in range(1, NZ)]
    peers += [net.dev(c=1 - net.c)]
    net.greet(peers)
    lanes = blk.shape[1]
    lanes_of(out, net.x, lanes)[...] = blk[...]
    n_all[net.y, net.z, net.c] = tails[...].astype(BF)
    half = lanes // 2
    cuts = {None: (0, lanes), 0: (0, half), 1: (half, half)}

    def part(at, h):
        first, width = cuts[h]
        return out.at[:, pl.ds(pl.multiple_of(at * lanes + first, half), width)]

    for _ in merge([ring(net, "x", part, lambda at: None, 0.0, 4.0), gather_small(net, n_all, pl.ds(0, 16), pl.ds(0, lanes), 0.0, 0.2)]):
        pass
    net.finish()


def back(blk, tails):
    lanes = blk.shape[1]
    vm = pl.BlockSpec(memory_space=pltpu.VMEM)
    return pl.pallas_call(
        back_kernel,
        out_shape=[
            jax.ShapeDtypeStruct((blk.shape[0], 4 * lanes), BF),
            jax.ShapeDtypeStruct((NY, NZ, 2, 16, lanes), BF),
        ],
        in_specs=[vm] * 2,
        out_specs=[vm] * 2,
        scratch_shapes=[
            pltpu.SemaphoreType.DMA((32,)),
            pltpu.SemaphoreType.DMA((32,)),
        ],
        compiler_params=pltpu.CompilerParams(collective_id=2, has_side_effects=True, vmem_limit_bytes=8 * 1024 * 1024),
        cost_estimate=pl.CostEstimate(flops=3 * 10**10, bytes_accessed=2**20, transcendentals=0),
        name="back",
    )(blk, tails)


def sums(lead, coef, aux, g_row, pall, x, pay, held):
    q = g_row.shape[1]
    coupled = aux.shape[1]
    modes = aux.shape[0] // (2 * held.shape[0])
    leads = q // coupled
    hot = [[jnp.where(lead[k] == l, 1.0, 0.0) for l in range(leads)] for k in range(modes)]
    level, width, re, im, occ = ([coef[i, k] for k in range(modes)] for i in range(5))

    def chunk(t, carry):
        rows = pl.ds(pl.multiple_of(32 * t, 32), 32)
        part = [aux[pl.ds(pl.multiple_of(32 * t * 2 * modes, 32) + i, 32, stride=2 * modes), :] for i in range(2 * modes)]
        pall[x, rows, :] = jnp.concatenate(part, axis=1).astype(BF)
        turned = []
        for k in range(modes):
            turned.append(-width[k] * part[2 * k] - level[k] * part[2 * k + 1])
            turned.append(level[k] * part[2 * k] - width[k] * part[2 * k + 1])

        def summed(values):
            out = []
            for p in range(2):
                for l in range(leads):
                    total = hot[0][l] * values[p]
                    for k in range(1, modes):
                        total = total + hot[k][l] * values[2 * k + p]
                    out.append(total)
            return jnp.concatenate(out, axis=1)

        l_sum = summed(part)
        held[rows, :] = l_sum.astype(BF)
        for i, a in enumerate((l_sum, summed(turned))):
            a = a.reshape(2, 2, 8, 2 * q).astype(BF)
            for c in range(2):
                pay[c, t // 4, pl.ds(2 * lax.rem(t, 4), 2), pl.ds(8 * i, 8), :] = a[:, c]
        return carry

    lax.fori_loop(0, held.shape[0] // 32, chunk, 0)
    n_re = dot(held[:, :q], g_row, 0, 0)
    n_im = -dot(held[:, q:], g_row, 0, 0)
    n = jnp.concatenate([n_re, n_im], axis=1).astype(BF)
    pay[0, :, :, 24:32, :] = n.reshape(NY, NZ, 8, 2 * q)
    lane = lax.broadcasted_iota(jnp.int32, (8, 2 * q), 1)
    scal = jnp.zeros((8, 2 * q), F32)
    for i, weights in enumerate((re, im, [re[k] * occ[k] for k in range(modes)], [im[k] * occ[k] for k in range(modes)])):
        for l in range(leads):
            scal = jnp.where(lane == i * leads + l, sum(weights[k] * hot[k][l] for k in range(modes)), scal)
    pay[1, :, :, 24:32, :] = jnp.broadcast_to(scal.astype(BF), (NY, NZ, 8, 2 * q))


def modes_kernel(lead, coef, aux, ham, ham2, pi, src, u, g, hg, out, hp, h2p, turned):
    k = pl.program_id(0)

    @pl.when(k == 0)
    def _():
        for i in range(0, ham2.shape[0], 512):
            turned[:, i : i + 512] = ham2[i : i + 512, :].T

    coupled = aux.shape[1]
    rows = ham.shape[0]
    modes = aux.shape[0] // (2 * rows)
    q = g.shape[1]
    hp[...] = dot(ham[...], pi[...])
    h2p[...] = dot(turned[...], pi[...])
    level, width, wr, wi, occ = (coef[i, k] for i in range(5))
    first = pl.multiple_of(lead[k] * coupled, coupled)
    re, im = pl.ds(first, coupled), pl.ds(pl.multiple_of(q + first, coupled), coupled)
    lr, li = -width, level
    ar, ai = 3 + 2 * H2 * lr, 2 * H2 * li
    cr = 3 * lr + 2 * H2 * (lr * lr - li * li)
    ci = 3 * li + 4 * H2 * lr * li
    er, ei = 4 * H2 * li, -3 - 4 * H2 * lr
    size = 64

    def chunk(t, carry):
        at = pl.ds(pl.multiple_of(size * t, size), size)
        gk, hgk = occ * g[at, re].astype(F32), 2 * H2 * occ * hg[at, re]
        br, bi = src[at, re] - gk, src[at, im] - gk
        tr = ar * br - ai * bi + u[at, re] - hgk
        ti = ar * bi + ai * br + u[at, im] + hgk
        start = pl.multiple_of(size * t * 2 * modes, size) + 2 * k
        at_re = pl.ds(start, size, stride=2 * modes)
        at_im = pl.ds(start + 1, size, stride=2 * modes)
        pr, pim = aux[at_re, :], aux[at_im, :]
        hr, hi = hp[at, :coupled], hp[at, coupled:]
        out[at_re, :] = cr * pr - ci * pim + er * hr - ei * hi - 2 * H2 * h2p[at, :coupled] + wr * tr - wi * ti
        out[at_im, :] = cr * pim + ci * pr + er * hi + ei * hr - 2 * H2 * h2p[at, coupled:] + wr * ti + wi * tr
        return carry

    lax.fori_loop(0, rows // size, chunk, 0)


def advance_modes(lead, coef, aux, ham, ham2, pi, src, u, g, hg):
    rows, n = ham.shape
    coupled = aux.shape[1]
    modes = aux.shape[0] // (2 * rows)
    sm = pl.BlockSpec(memory_space=pltpu.SMEM)

    def whole(a):
        return pl.BlockSpec(a.shape, lambda k: (0,) * a.ndim)

    return pl.pallas_call(
        modes_kernel,
        grid=(modes,),
        out_shape=jax.ShapeDtypeStruct(aux.shape, F32),
        in_specs=[sm, sm, whole(aux), whole(ham), whole(ham2), pl.BlockSpec((n, 2 * coupled), lambda k: (0, k))]
        + [whole(a) for a in (src, u, g, hg)],
        out_specs=whole(aux),
        scratch_shapes=[pltpu.VMEM((rows, 2 * coupled), F32)] * 2 + [pltpu.VMEM((rows, n), BF)],
        compiler_params=pltpu.CompilerParams(vmem_limit_bytes=28 * 1024 * 1024),
        cost_estimate=pl.CostEstimate(flops=4 * rows * n * 2 * coupled * modes, bytes_accessed=16 * 1024 * 1024, transcendentals=0),
        name="modes",
    )(lead, coef, aux, ham, ham2, pi, src, u, g, hg)


def by_lead(x, gamma):
    leads, coupled = gamma.shape[:2]
    return jnp.concatenate(
        [dot(x[:, l * coupled : (l + 1) * coupled], gamma[l]) for l in range(leads)], axis=1
    )


def shards(density, auxiliary, hamiltonian, coupling, lead_index, mode_level, mode_width, residue, occupation, lead_gamma):
    rows, cols = density.shape[1:]
    n = hamiltonian.shape[1]
    leads, coupled = coupling.shape
    q = leads * coupled
    modes = auxiliary.shape[1]
    n_mode = lax.axis_size("mode")
    n_row = lax.axis_size("row")
    x_pos, m_pos = lax.axis_index("row"), lax.axis_index("mode")
    row_start, col_start = x_pos * rows, m_pos * cols
    flat = coupling.reshape(-1)

    e_row = (row_start + jnp.arange(rows, dtype=jnp.int32)[:, None] == flat[None, :]).astype(BF)
    e_col = (col_start + jnp.arange(cols, dtype=jnp.int32)[:, None] == flat[None, :]).astype(BF)
    rho_t = jnp.swapaxes(density, 1, 2).astype(BF).reshape(2 * cols, rows)
    ham_ct = jnp.swapaxes(lax.dynamic_slice_in_dim(hamiltonian, col_start, cols, 1), 0, 1)

    coef = jnp.stack([mode_level, mode_width, residue[:, 0], residue[:, 1], occupation])
    aux = auxiliary.reshape(-1, coupled)
    blk = jnp.concatenate([ham_ct, rho_t], axis=0).reshape(3, cols, rows)
    first, hrho_t, ham2_c, pi_all, panel, ham2_all, whole, tails, scal, grow_full, he_row_b, hg_row, he_col = front(
        lead_index, coef, aux, blk, hamiltonian, flat[None], lead_gamma
    )
    g_row = lax.dynamic_slice_in_dim(grow_full, row_start, rows, 0)
    ham_c = first[0]
    piece = rows // n_mode
    pi_all = pi_all.reshape(n, -1)
    panel = panel.reshape(2, n, rows)
    ham2_all = ham2_all.reshape(n, rows)
    whole = whole.reshape(n_mode, 2 * piece, 2 * q)
    l1_b = whole[:, :piece].reshape(rows, 2 * q)
    m1 = whole[:, piece : 2 * piece].reshape(rows, 2 * q).astype(F32)
    scal = scal[0]
    w_sum, v_sum = scal[: 2 * leads], scal[2 * leads : 4 * leads]

    src = dot(panel, grow_full, 1, 0)
    src = jnp.concatenate([src[0], src[1]], axis=1)
    w_q = jnp.repeat(w_sum, coupled)
    v_q = jnp.repeat(v_sum, coupled)
    s_re, s_im = src[:, :q], src[:, q:]
    g_row_f = g_row.astype(F32)
    drive = jnp.concatenate(
        [w_q[:q] * s_re - w_q[q:] * s_im - (v_q[:q] - v_q[q:]) * g_row_f, w_q[:q] * s_im + w_q[q:] * s_re - (v_q[:q] + v_q[q:]) * g_row_f], axis=1
    )
    x_row = (3.0 * l1_b.astype(F32) + 2 * H2 * (m1 + drive)).astype(BF)
    p1 = jnp.concatenate([dot(e_col, l1_b[:, p * q : (p + 1) * q], 1, 1) for p in range(2)], 0)
    xe = jnp.concatenate([dot(e_col, x_row[:, p * q : (p + 1) * q], 1, 1) for p in range(2)], 0)
    rhoh_t = jnp.swapaxes(dot(jnp.concatenate([ham_c, ham2_c], 0), panel, 1, 1), 0, 1)
    rhoh_t, rhoh2_t = (rhoh_t[:, i * cols : (i + 1) * cols].reshape(2 * cols, rows) for i in range(2))
    y = hrho_t - 2.0 * rhoh_t + 2.0 * jnp.concatenate([-p1[cols:], p1[:cols]], 0)
    z = dot(lax.dynamic_slice_in_dim(ham_c, row_start, rows, 1), l1_b)
    owner = col_start // rows
    own_l = lax.dynamic_slice_in_dim(l1_b, col_start - owner * rows, cols, 0)
    own_x = lax.dynamic_slice_in_dim(x_row, col_start - owner * rows, cols, 0)
    mask = (x_pos == owner).astype(BF)
    second, n_all = back(jnp.concatenate([y.astype(BF), z.astype(BF), own_l * mask, own_x * mask], 0), tails)
    f_all = n_all[..., :8, :].reshape(rows, 2 * q).astype(F32)
    n_all = n_all[:, :, 0, 8:].reshape(q, 2 * q)
    third = second[2 * cols :].astype(F32)
    third = sum(third[:, i * rows : (i + 1) * rows] for i in range(n_row))
    z, l_c, x_c = third[:cols], third[cols : 2 * cols], third[2 * cols :]
    hy = dot(second[: 2 * cols], hamiltonian, 1, 1)
    b_re = x_c[:, :q] + 4 * H2 * z[:, q:]
    b_im = -x_c[:, q:] + 4 * H2 * z[:, :q]
    back_re = dot(b_re.astype(BF), e_row, 1, 1)
    back_im = dot(b_im.astype(BF), e_row, 1, 1)
    l_cb = l_c.astype(BF)
    c1_re, c1_im = dot(l_cb[:, :q], he_row_b, 1, 1), -dot(l_cb[:, q:], he_row_b, 1, 1)
    c2_re, c2_im = dot(he_col, l1_b[:, :q], 1, 1), dot(he_col, l1_b[:, q:], 1, 1)
    d_re, d_im = c1_re - c2_re, c1_im - c2_im
    comm = hrho_t - rhoh_t
    base = -2 * H2 * (hy + rhoh2_t) + xe
    out_re = 3.0 * comm[cols:] + base[:cols] + back_re + 2 * H2 * d_im
    out_im = -3.0 * comm[:cols] + base[cols:] + back_im - 2 * H2 * d_re
    density_rate = jnp.swapaxes(jnp.stack([out_re, out_im]), 1, 2)

    lg = jnp.concatenate([by_lead(l1_b[:, p * q : (p + 1) * q], lead_gamma) for p in range(2)], 1)
    u = 2 * H2 * (f_all + lg + dot(e_row, n_all))
    auxiliary_rate = advance_modes(
        lead_index, coef, aux, hamiltonian, ham2_all, pi_all, src, u, g_row, hg_row
    ).reshape(auxiliary.shape)
    return density_rate, auxiliary_rate


def solution(mesh):
    in_specs = (
        P(None, "row", "mode"),
        P("row", "mode", None, None),
        P("row", None),
        P(),
        P("mode"),
        P("mode"),
        P("mode"),
        P("mode", None),
        P("mode"),
        P(),
    )
    out_specs = (P(None, "row", "mode"), P("row", "mode", None, None))
    return jax.shard_map(shards, mesh=mesh, in_specs=in_specs, out_specs=out_specs, check_vma=False)
```

time: 152 us -> 116 us (0.76)
  Pallas kernels: 111 us -> 97.9 us
  matrix products: 19 us -> 6.11 us
  local copies, waits for them, and re-layouts: 16.6 us -> 8.28 us
    pallas_call x4 -> x2, Pallas kernels: 102 us -> 87.8 us  [the longest x1 68.9 us: front(): pl.pallas_call(front_kernel, out_shape=[jax.ShapeDtypeStruct((3, cols, n)...]
    dot_general x38 -> x19, matrix products: 19 us -> 6.11 us  [dot(): lax.dot_general(a, b, (((ca,), (cb,)), ((), ())), preferred_element_type=...]
    slice x6 -> x3, local copies, waits for them, and re-layouts: 6.27 us -> 0.08 us  [the longest x1 0.04 us: shards(): f_all = n_all[..., :8, :].reshape(rows, 2 * q).astype(F32)]
    another operation x1 -> x0, local copies, waits for them, and re-layouts: 3.96 us -> none  [shards(): ham2_all = panel[:, 2].reshape(n, rows)]
    unnamed x80 -> x18, local copies, waits for them, and re-layouts: 5.92 us -> 5.38 us
where the time goes in v3:
time: 116 us
  Pallas kernels  97.9 us (84%)
  local copies, waits for them, and re-layouts  8.28 us (7%)
  matrix products  6.11 us (5%)
  other arithmetic  2.52 us (2%)
    pallas_call x1, Pallas kernels, front(): pl.pallas_call(front_kernel, out_shape=[jax.ShapeDtypeStruct((3, cols, n)...  68.9 us
    pallas_call x1, Pallas kernels, back(): pl.pallas_call(back_kernel, out_shape=[jax.ShapeDtypeStruct((blk.shape[0]...  18.9 us
    pallas_call x1, Pallas kernels, advance_modes(): pl.pallas_call(modes_kernel, grid=(modes,), out_shape=jax.ShapeDtypeStruc...  10.1 us
    dot_general x19, matrix products, dot(): lax.dot_general(a, b, (((ca,), (cb,)), ((), ())), preferred_element_type=...  6.11 us
    unnamed x18, local copies, waits for them, and re-layouts  5.38 us

profile of v3, /device:TPU:1, one launch (start us, length us, event | category | flops | bytes accessed | tf_op | source)
XLA Modules:
  0.0 115.8 jit_solution(14312616573478556150)
XLA Ops:
  0.7 0.8 slice_bitcast_fusion.6
  1.4 0.7 stack.24.coef
  2.1 0.9 convert_element_type.48
  3.1 1.0 dynamic-slice_bitcast_fusion
  4.2 1.6 %copy-done = bf16[512,2048]{1,0:T(8,128)(2,1)S(1)} copy-done((bf16[512,2048]{1,0:T(8,128)(2,1)S(1)}, bf16[512,2048]{1,0:T(8,128)(2,1)}, u32[]{:S(2)}) %copy-start) | copy-done | bytes 2097176
  5.8 0.8 copy-done.2
  6.6 0.7 copy-done.3
  7.3 1.6 %copy-done.5 = f32[512,4,2,128]{3,2,1,0:T(2,128)S(1)} copy-done((f32[512,4,2,128]{3,2,1,0:T(2,128)S(1)}, f32[512,4,2,128]{3,2,1,0:T(2,128)}, u32[]{:S(2)}) %copy-start.5) | copy-done | bytes 2097176
  8.9 0.7 copy-done.7
  9.5 68.9 %front.1 = (bf16[3,32,2048]{2,1,0:T(8,128)(2,1)S(1)}, f32[64,512]{1,0:T(8,128)S(1)}, bf16[32,2048]{1,0:T(8,128)(2,1)S(1)}, bf16[4,512,1024]{2,1,0:T(8,128)(2,1)S...) custom-call(s32[4]{0:T(128)S(1)} %copy-done.7, ...), custom_call_target="tpu_custom_call" | custom-call | flops 99999997952 | bytes 16777216 | tf_op jit(solution)/shard_map/front/pallas_call | solution.py:350
  78.7 0.8 convolution_bitcast_fusion
  79.5 1.3 %fusion.12 = f32[2,512,256]{2,1,0:T(8,128)S(1)} fusion(bf16[2,2048,512]{2,1,0:T(8,128)(2,1)S(1)} %bitcast.108, bf16[2048,256]{1,0:T(8,128)(2,1)S(1)} %get-tuple-element.23), kind=kOutput, calls=%fused_computation.25 | convolution fusion | flops 1073741824 | bytes 6291456 | tf_op jit(solution)/shard_map/dot_general | solution.py:14
  81.0 0.2 convolution_convert_fusion
  81.3 0.2 fusion.11
  81.9 0.2 fusion.33
  82.1 0.2 convolution_negate_fusion.1
  82.3 0.2 fusion.19
  82.5 0.2 fusion.21
  82.7 0.2 fusion.37
  83.1 0.2 fusion.41
  83.2 0.2 fusion.43
  83.4 18.9 %back.1 = (bf16[160,2048]{1,0:T(8,128)(2,1)S(1)}, bf16[4,8,2,16,512]{4,3,2,1,0:T(8,128)(2,1)S(1)}) custom-call(bf16[160,512]{1,0:T(8,128)(2,1)S(1)} %pad_maximum_fusion.1.blk, f32[16,512]{1,0:T(8,128)S(1)} %get-tuple-element.24.tails), custom_call_target="tpu_custom_call" | custom-call | flops 30000001024 | bytes 1048576 | tf_op jit(solution)/shard_map/back/pallas_call | solution.py:414
  102.3 0.8 fusion.2
  103.3 0.2 fusion.68
  103.4 0.2 convolution_negate_fusion
  103.6 0.2 fusion.7
  103.8 0.2 fusion.8
  104.0 0.3 fusion.4
  104.3 0.3 fusion.6
  104.6 0.7 maximum_bitcast_fusion.2
  105.3 0.4 fusion.u
  105.7 10.1 %modes.1 = f32[4096,128]{1,0:T(8,128)} custom-call(s32[4]{0:T(128)S(1)} %copy-done.8, f32[5,4]{1,0:T(8,128)S(1)} %stack.24.coef, f32[4096,128]{1,0:T(8,128)S(1)} %bitcast.122, bf16[512,2048]{1,0:T(8,128)(2,1)S(1)} %copy-done.1, bf16[2048,512]{1,0:T(8,128)(2,1)S(1)} %bitcast.124, bf16[2048,1024]{1,0:T(8,128)(2,1)S(1)} %bitcast.123, ...), custom_call_target="tpu_custom_call" | custom-call | flops 4294967296 | bytes 16777216 | tf_op jit(solution)/shard_map/modes/pallas_call | solution.py:531
  (36 shorter events, 1.3 us)
Async XLA Ops:
  4.2 1.6 %copy-start = (bf16[512,2048]{1,0:T(8,128)(2,1)S(1)}, bf16[512,2048]{1,0:T(8,128)(2,1)}, u32[]{:S(2)}) copy-start(bf16[512,2048]{1,0:T(8,128)(2,1)} %ham.3) | copy-start | bytes 6291460
  5.8 0.8 copy-start.2
  6.6 0.7 copy-start.3
  7.3 1.6 %copy-start.5 = (f32[512,4,2,128]{3,2,1,0:T(2,128)S(1)}, f32[512,4,2,128]{3,2,1,0:T(2,128)}, u32[]{:S(2)}) copy-start(f32[512,4,2,128]{3,2,1,0:T(2,128)} %param.11) | copy-start | bytes 6291460
  8.9 0.7 copy-start.7
  102.3 1.7 %copy-start.4 = (s32[2,128]{1,0:T(2,128)S(1)}, s32[2,128]{1,0:T(2,128)}, u32[]{:S(2)}) copy-start(s32[2,128]{1,0:T(2,128)} %param.13) | copy-start | bytes 3076
  103.2 2.5 %copy-start.1 = (bf16[512,2048]{1,0:T(8,128)(2,1)S(1)}, bf16[512,2048]{1,0:T(8,128)(2,1)}, u32[]{:S(2)}) copy-start(bf16[512,2048]{1,0:T(8,128)(2,1)} %ham.3) | copy-start | bytes 6291460
  103.2 2.5 %copy-start.6 = (f32[512,4,2,128]{3,2,1,0:T(2,128)S(1)}, f32[512,4,2,128]{3,2,1,0:T(2,128)}, u32[]{:S(2)}) copy-start(f32[512,4,2,128]{3,2,1,0:T(2,128)} %param.11) | copy-start | bytes 6291460
  103.2 2.5 %copy-start.8 = (s32[4]{0:T(128)S(1)}, s32[4]{0:T(128)}, u32[]{:S(2)}) copy-start(s32[4]{0:T(128)} %lead.3) | copy-start | bytes 52

commit v4 on v3

--- a/solution.py
+++ b/solution.py
@@ -148,6 +148,32 @@
         net.arrive(ref, slot)
 
 
+def gather_small_turned(net, whole, rows, lanes, t, unit):
+    c = net.c
+    cuts = {None: lanes, 0: pl.ds(lanes.start, lanes.size // 2), 1: pl.ds(lanes.start + lanes.size // 2, lanes.size // 2)}
+    yield from ring(net, "y", lambda p, h: whole.at[p, net.z, c, rows, cuts[h]], lambda at: None, t, 2.2)
+    slots = [net.slot() for _ in range(NZ - 1)]
+    mine = whole.at[:, net.z, c, rows, lanes]
+    for d in (4, 3, 5, 2, 6, 1, 7):
+        net.start(mine, mine, net.dev(z=net.at("z", d)), slots[d - 1])
+    waits = []
+
+    def share(pos):
+        slot = net.slot()
+        ref = whole.at[:, pos, c, rows, lanes]
+        net.start(ref, ref, net.dev(c=1 - c), slot)
+        waits.append((whole.at[:, pos, 1 - c, rows, lanes], slot))
+
+    share(net.z)
+    for d in (1, 7, 2, 6, 3, 5, 4):
+        yield t + 7.0 + min(d, NZ - d) + 10 * unit
+        net.arrive(whole.at[:, net.at("z", -d), c, rows, lanes], slots[d - 1])
+        share(net.at("z", -d))
+    yield t + 13.0 + 10 * unit
+    for ref, slot in waits:
+        net.arrive(ref, slot)
+
+
 def merge(threads):
     live = []
     for thread in threads:
@@ -164,17 +190,17 @@
             live[0][0] = when
 
 
-def reduce_plane(net, chain, pay, whole, tails, scal, xs, pair, acc, got1, got2, gotz, t):
+def reduce_plane(net, chain, pay, pair, acc, got1, got2, gotz, t, done):
     c, y, z = net.c, net.y, net.z
-    width = got2.shape[-1]
-    ln = pl.ds(chain * width, width)
+    count = got2.shape[-2]
+    rw = pl.ds(chain * count, count)
     slot = net.slot()
-    net.start(pay.at[1 - c, :, :, :, ln], pair.at[:, :, :, ln], net.dev(c=1 - c), slot)
+    net.start(pay.at[1 - c, :, :, rw, :], pair.at[:, :, rw, :], net.dev(c=1 - c), slot)
     yield t + 2.0
-    net.arrive(pair.at[:, :, :, ln], slot)
+    net.arrive(pair.at[:, :, rw, :], slot)
 
     def add_pair(i, carry):
-        acc[i, :, :, ln] = (pay[c, i, :, :, ln].astype(F32) + pair[i, :, :, ln].astype(F32)).astype(BF)
+        acc[i, :, rw, :] = (pay[c, i, :, rw, :].astype(F32) + pair[i, :, rw, :].astype(F32)).astype(BF)
         return carry
 
     lax.fori_loop(0, NY, add_pair, 0)
@@ -185,45 +211,43 @@
         s_of_f = lax.rem(y + 2, NY)
         zs = pl.ds(color * half, half)
         slots = [net.slot() for _ in range(3)]
-        net.start(acc.at[s_of_f, zs, :, ln], got1.at[chain, color, 1], net.dev(y=f), slots[1])
-        net.start(acc.at[f, zs, :, ln], got1.at[chain, color, 0], net.dev(y=f), slots[0])
+        net.start(acc.at[s_of_f, zs, rw, :], got1.at[chain, color, 1], net.dev(y=f), slots[1])
+        net.start(acc.at[f, zs, rw, :], got1.at[chain, color, 0], net.dev(y=f), slots[0])
         colors.append((f, s, zs, slots))
     yield t + 5.5
     for color, (f, s, zs, slots) in enumerate(colors):
         net.arrive(got1.at[chain, color, 1], slots[1])
-        acc[s, zs, :, ln] = (acc[s, zs, :, ln].astype(F32) + got1[chain, color, 1].astype(F32)).astype(BF)
-        net.start(acc.at[s, zs, :, ln], got2.at[chain, color], net.dev(y=s), slots[2])
+        acc[s, zs, rw, :] = (acc[s, zs, rw, :].astype(F32) + got1[chain, color, 1].astype(F32)).astype(BF)
+        net.start(acc.at[s, zs, rw, :], got2.at[chain, color], net.dev(y=s), slots[2])
     yield t + 9.5
     for color, (f, s, zs, slots) in enumerate(colors):
         net.arrive(got1.at[chain, color, 0], slots[0])
         net.arrive(got2.at[chain, color], slots[2])
-        total = acc[y, zs, :, ln].astype(F32) + got1[chain, color, 0].astype(F32) + got2[chain, color].astype(F32)
-        acc[y, zs, :, ln] = total.astype(BF)
+        total = acc[y, zs, rw, :].astype(F32) + got1[chain, color, 0].astype(F32) + got2[chain, color].astype(F32)
+        acc[y, zs, rw, :] = total.astype(BF)
     zslots = [net.slot() for _ in range(NZ - 1)]
     for d in (4, 3, 5, 2, 6, 1, 7):
-        net.start(acc.at[y, net.at("z", d), :, ln], gotz.at[chain, d - 1], net.dev(z=net.at("z", d)), zslots[d - 1])
+        net.start(acc.at[y, net.at("z", d), rw, :], gotz.at[chain, d - 1], net.dev(z=net.at("z", d)), zslots[d - 1])
     yield t + 16.0
-    total = acc[y, z, :, ln].astype(F32)
+    total = acc[y, z, rw, :].astype(F32)
     for d in range(1, NZ):
         net.arrive(gotz.at[chain, d - 1], zslots[d - 1])
         total = total + gotz[chain, d - 1].astype(F32)
-    whole[y, z, c, :, ln] = total[:16].astype(BF)
-    tails[pl.ds(0, 8), ln] = total[16:24]
-    xs[0, :, ln] = total[24:]
+    yield from done(total, t + 16.0)
+
+
+def small_ends(net, total, tails, scal, xs, t):
+    tails[0:8] = total[0:8]
+    xs[0] = total[8:16]
     slots = [net.slot() for _ in range(4)]
-    mine = xs.at[0, :, ln]
-    net.start(mine, xs.at[4, :, ln], net.dev(c=1 - c), slots[0])
+    net.start(xs.at[0], xs.at[4], net.dev(c=1 - net.c), slots[0])
     for d in (1, 2, 3):
-        net.start(mine, xs.at[d, :, ln], net.dev(x=net.at("x", d)), slots[d])
-
-    def small_ends():
-        yield t + 34.0
-        for d, slot in zip((4, 1, 2, 3), slots):
-            net.arrive(xs.at[d, :, ln], slot)
-        tails[pl.ds(8, 8), ln] = xs[0, :, ln] + xs[1, :, ln] + xs[2, :, ln] + xs[3, :, ln]
-        scal[:, ln] = jnp.where(jnp.full((8, width), c) == 1, xs[0, :, ln], xs[4, :, ln])
-
-    yield from merge([gather_small(net, whole, pl.ds(0, 16), ln, t + 16.0, 0.2), small_ends()])
+        net.start(xs.at[0], xs.at[d], net.dev(x=net.at("x", d)), slots[d])
+    yield t + 18.0
+    for d, slot in zip((4, 1, 2, 3), slots):
+        net.arrive(xs.at[d], slot)
+    tails[8:16] = xs[0] + xs[1] + xs[2] + xs[3]
+    scal[...] = jnp.where(jnp.full(scal.shape, net.c) == 1, xs[0], xs[4])
 
 
 def gather_rows(net, pall):
@@ -294,14 +318,25 @@
         sums(lead, coef, aux, g_row, pall, x, pay, held)
         rows_thread = gather_rows(net, pall)
         start = next(rows_thread)
-        yield from merge([more(), resumed(rows_thread, start)])
+        chain = reduce_plane(net, 0, pay, pair, acc, got1, got2, gotz, 6.0, gather_sums)
+        yield from merge([chain, more(), resumed(rows_thread, start)])
+
+    def gather_sums(total, t):
+        whole[y, z, c] = total.astype(BF)
+        lanes = total.shape[1]
+        yield from gather_small(net, whole, pl.ds(0, 16), pl.ds(0, lanes), t, 0.35)
+
+    def send_ends(total, t):
+        yield from small_ends(net, total, tails, scal, xs, t)
 
     def more():
-        yield 9.0
+        yield 7.0
         arrived()
         applied = dot(first[...].reshape(3 * cols, -1), ham[...], 1, 1)
         own2[...] = applied[:cols].astype(BF)
         ham2[0, y, z, c] = own2[...]
+        turns = gather_plane(net, ham2, 9.0, 0.4)
+        turn = next(turns)
         hrho[...] = applied[cols:]
         hg = dot(first[0], grow[...]).astype(BF)
         lhs = jnp.concatenate([applied[cols:].astype(BF), blk[1:].reshape(2 * cols, rows)], axis=0)
@@ -314,9 +349,9 @@
             f = f.astype(BF).reshape(NY, NZ, 2, 8, q)
             for cc in range(2):
                 pay[cc, :, :, 16:24, i * q : (i + 1) * q] = f[:, :, cc]
-        chains = [reduce_plane(net, i, pay, whole, tails, scal, xs, pair, acc, got1, got2, gotz, 10.0 + 3.0 * i) for i in range(2)]
+        chain = reduce_plane(net, 1, pay, pair, acc, got1, got2, gotz, 11.0, send_ends)
         spread = spread_ham2()
-        yield from merge([*chains, gather_plane(net, ham2, 11.0, 0.4), spread, spare()])
+        yield from merge([chain, resumed(turns, turn), spread, spare()])
 
     def spare():
         yield 13.8
@@ -342,7 +377,6 @@
 
 def front(lead, coef, aux, blk, ham, flat, gamma):
     cols, lanes = blk.shape[1:]
-    half = lanes // 2
     n = ham.shape[1]
     vm = pl.BlockSpec(memory_space=pltpu.VMEM)
     sm = pl.BlockSpec(memory_space=pltpu.SMEM)
@@ -374,9 +408,9 @@
             pltpu.VMEM((lanes, lanes), BF),
             pltpu.VMEM((NY, NZ, 32, lanes), BF),
             pltpu.VMEM((NY, NZ, 32, lanes), BF),
-            pltpu.VMEM((2, 2, 2, NZ // 2, 32, half), BF),
-            pltpu.VMEM((2, 2, NZ // 2, 32, half), BF),
-            pltpu.VMEM((2, NZ - 1, 32, half), BF),
+            pltpu.VMEM((2, 2, 2, NZ // 2, 16, lanes), BF),
+            pltpu.VMEM((2, 2, NZ // 2, 16, lanes), BF),
+            pltpu.VMEM((2, NZ - 1, 16, lanes), BF),
             pltpu.SemaphoreType.DMA((sems,)),
             pltpu.SemaphoreType.DMA((sems,)),
         ],
@@ -403,7 +437,11 @@
         first, width = cuts[h]
         return out.at[:, pl.ds(pl.multiple_of(at * lanes + first, half), width)]
 
-    for _ in merge([ring(net, "x", part, lambda at: None, 0.0, 4.0), gather_small(net, n_all, pl.ds(0, 16), pl.ds(0, lanes), 0.0, 0.2)]):
+    for _ in merge([
+        gather_small(net, n_all, pl.ds(0, 16), pl.ds(0, half), 0.0, 0.2),
+        gather_small_turned(net, n_all, pl.ds(0, 16), pl.ds(half, half), 0.0, 0.3),
+        ring(net, "x", part, lambda at: None, 0.0, 4.0),
+    ]):
         pass
     net.finish()
 
@@ -420,8 +458,8 @@
         in_specs=[vm] * 2,
         out_specs=[vm] * 2,
         scratch_shapes=[
-            pltpu.SemaphoreType.DMA((32,)),
-            pltpu.SemaphoreType.DMA((32,)),
+            pltpu.SemaphoreType.DMA((48,)),
+            pltpu.SemaphoreType.DMA((48,)),
         ],
         compiler_params=pltpu.CompilerParams(collective_id=2, has_side_effects=True, vmem_limit_bytes=8 * 1024 * 1024),
         cost_estimate=pl.CostEstimate(flops=3 * 10**10, bytes_accessed=2**20, transcendentals=0),

time: 116 us -> 111 us (0.957)
  Pallas kernels: 97.9 us -> 93.3 us
    pallas_call x1, Pallas kernels: 68.9 us -> 62.9 us  [front(): pl.pallas_call(front_kernel, out_shape=[jax.ShapeDtypeStruct((3, cols, n)...]
    pallas_call x1, Pallas kernels: 18.9 us -> 20.3 us  [back(): pl.pallas_call(back_kernel, out_shape=[jax.ShapeDtypeStruct((blk.shape[0]...]
where the time goes in v4:
time: 111 us
  Pallas kernels  93.3 us (84%)
  local copies, waits for them, and re-layouts  8.28 us (7%)
  matrix products  6.12 us (6%)
  other arithmetic  2.52 us (2%)
    pallas_call x1, Pallas kernels, front(): pl.pallas_call(front_kernel, out_shape=[jax.ShapeDtypeStruct((3, cols, n)...  62.9 us
    pallas_call x1, Pallas kernels, back(): pl.pallas_call(back_kernel, out_shape=[jax.ShapeDtypeStruct((blk.shape[0]...  20.3 us
    pallas_call x1, Pallas kernels, advance_modes(): pl.pallas_call(modes_kernel, grid=(modes,), out_shape=jax.ShapeDtypeStruc...  10.1 us
    dot_general x19, matrix products, dot(): lax.dot_general(a, b, (((ca,), (cb,)), ((), ())), preferred_element_type=...  6.12 us
    unnamed x18, local copies, waits for them, and re-layouts  5.38 us

profile of v4, /device:TPU:1, one launch (start us, length us, event | category | flops | bytes accessed | tf_op | source)
XLA Modules:
  0.0 111.2 jit_solution(10098916481413194079)
XLA Ops:
  0.7 0.8 slice_bitcast_fusion.6
  1.4 0.7 stack.24.coef
  2.1 0.9 convert_element_type.48
  3.1 1.0 dynamic-slice_bitcast_fusion
  4.2 1.6 %copy-done = bf16[512,2048]{1,0:T(8,128)(2,1)S(1)} copy-done((bf16[512,2048]{1,0:T(8,128)(2,1)S(1)}, bf16[512,2048]{1,0:T(8,128)(2,1)}, u32[]{:S(2)}) %copy-start) | copy-done | bytes 2097176
  5.8 0.8 copy-done.2
  6.6 0.7 copy-done.3
  7.3 1.6 %copy-done.5 = f32[512,4,2,128]{3,2,1,0:T(2,128)S(1)} copy-done((f32[512,4,2,128]{3,2,1,0:T(2,128)S(1)}, f32[512,4,2,128]{3,2,1,0:T(2,128)}, u32[]{:S(2)}) %copy-start.5) | copy-done | bytes 2097176
  8.9 0.7 copy-done.7
  9.5 62.9 %front.1 = (bf16[3,32,2048]{2,1,0:T(8,128)(2,1)S(1)}, f32[64,512]{1,0:T(8,128)S(1)}, bf16[32,2048]{1,0:T(8,128)(2,1)S(1)}, bf16[4,512,1024]{2,1,0:T(8,128)(2,1)S...) custom-call(s32[4]{0:T(128)S(1)} %copy-done.7, ...), custom_call_target="tpu_custom_call" | custom-call | flops 99999997952 | bytes 16777216 | tf_op jit(solution)/shard_map/front/pallas_call | solution.py:384
  72.7 0.8 convolution_bitcast_fusion
  73.5 1.3 %fusion.12 = f32[2,512,256]{2,1,0:T(8,128)S(1)} fusion(bf16[2,2048,512]{2,1,0:T(8,128)(2,1)S(1)} %bitcast.108, bf16[2048,256]{1,0:T(8,128)(2,1)S(1)} %get-tuple-element.23), kind=kOutput, calls=%fused_computation.25 | convolution fusion | flops 1073741824 | bytes 6291456 | tf_op jit(solution)/shard_map/dot_general | solution.py:14
  75.0 0.2 convolution_convert_fusion
  75.3 0.2 fusion.11
  75.9 0.2 fusion.33
  76.1 0.2 convolution_negate_fusion.1
  76.3 0.2 fusion.19
  76.5 0.2 fusion.21
  76.7 0.2 fusion.37
  77.0 0.2 fusion.41
  77.2 0.2 fusion.43
  77.4 20.3 %back.1 = (bf16[160,2048]{1,0:T(8,128)(2,1)S(1)}, bf16[4,8,2,16,512]{4,3,2,1,0:T(8,128)(2,1)S(1)}) custom-call(bf16[160,512]{1,0:T(8,128)(2,1)S(1)} %pad_maximum_fusion.1.blk, f32[16,512]{1,0:T(8,128)S(1)} %get-tuple-element.24.tails), custom_call_target="tpu_custom_call" | custom-call | flops 30000001024 | bytes 1048576 | tf_op jit(solution)/shard_map/back/pallas_call | solution.py:452
  97.7 0.8 fusion.2
  98.6 0.2 fusion.68
  98.8 0.2 convolution_negate_fusion
  99.0 0.2 fusion.7
  99.2 0.2 fusion.8
  99.4 0.3 fusion.4
  99.7 0.3 fusion.6
  100.0 0.7 maximum_bitcast_fusion.2
  100.7 0.4 fusion.u
  101.1 10.1 %modes.1 = f32[4096,128]{1,0:T(8,128)} custom-call(s32[4]{0:T(128)S(1)} %copy-done.8, f32[5,4]{1,0:T(8,128)S(1)} %stack.24.coef, f32[4096,128]{1,0:T(8,128)S(1)} %bitcast.122, bf16[512,2048]{1,0:T(8,128)(2,1)S(1)} %copy-done.1, bf16[2048,512]{1,0:T(8,128)(2,1)S(1)} %bitcast.124, bf16[2048,1024]{1,0:T(8,128)(2,1)S(1)} %bitcast.123, ...), custom_call_target="tpu_custom_call" | custom-call | flops 4294967296 | bytes 16777216 | tf_op jit(solution)/shard_map/modes/pallas_call | solution.py:569
  (36 shorter events, 1.3 us)
Async XLA Ops:
  4.2 1.6 %copy-start = (bf16[512,2048]{1,0:T(8,128)(2,1)S(1)}, bf16[512,2048]{1,0:T(8,128)(2,1)}, u32[]{:S(2)}) copy-start(bf16[512,2048]{1,0:T(8,128)(2,1)} %ham.3) | copy-start | bytes 6291460
  5.8 0.8 copy-start.2
  6.6 0.7 copy-start.3
  7.3 1.6 %copy-start.5 = (f32[512,4,2,128]{3,2,1,0:T(2,128)S(1)}, f32[512,4,2,128]{3,2,1,0:T(2,128)}, u32[]{:S(2)}) copy-start(f32[512,4,2,128]{3,2,1,0:T(2,128)} %param.11) | copy-start | bytes 6291460
  8.9 0.7 copy-start.7
  97.7 1.7 %copy-start.4 = (s32[2,128]{1,0:T(2,128)S(1)}, s32[2,128]{1,0:T(2,128)}, u32[]{:S(2)}) copy-start(s32[2,128]{1,0:T(2,128)} %param.13) | copy-start | bytes 3076
  98.5 2.5 %copy-start.1 = (bf16[512,2048]{1,0:T(8,128)(2,1)S(1)}, bf16[512,2048]{1,0:T(8,128)(2,1)}, u32[]{:S(2)}) copy-start(bf16[512,2048]{1,0:T(8,128)(2,1)} %ham.3) | copy-start | bytes 6291460
  98.5 2.5 %copy-start.6 = (f32[512,4,2,128]{3,2,1,0:T(2,128)S(1)}, f32[512,4,2,128]{3,2,1,0:T(2,128)}, u32[]{:S(2)}) copy-start(f32[512,4,2,128]{3,2,1,0:T(2,128)} %param.11) | copy-start | bytes 6291460
  98.6 2.5 %copy-start.8 = (s32[4]{0:T(128)S(1)}, s32[4]{0:T(128)}, u32[]{:S(2)}) copy-start(s32[4]{0:T(128)} %lead.3) | copy-start | bytes 52

commit v5 on v4

--- a/solution.py
+++ b/solution.py
@@ -420,7 +420,25 @@
     )(lead, coef, aux, blk, ham, flat, gamma)
 
 
-def back_kernel(blk, tails, out, n_all, send, recv):
+def products(ham, ham2, pi, hp, h2p, turned):
+    size, deep = 256, 512
+    pieces = pi.shape[1] // size
+
+    def turn(i):
+        turned[:, i * deep : (i + 1) * deep] = ham2[i * deep : (i + 1) * deep, :].T
+
+    def times(left, out, k):
+        out[:, k * size : (k + 1) * size] = dot(left[...], pi[:, k * size : (k + 1) * size])
+
+    steps = [lambda k=k: times(ham, hp, k) for k in range(pieces)]
+    steps += [lambda i=i: turn(i) for i in range(ham2.shape[0] // deep)]
+    steps += [lambda k=k: times(turned, h2p, k) for k in range(pieces)]
+    for step, t in zip(steps, (0.5, 0.6, 0.7, 2.3, 2.4, 4.5, 4.6, 4.7, 6.1, 6.2, 8.1, 9.5)):
+        yield t
+        step()
+
+
+def back_kernel(blk, tails, ham, ham2, pi, out, n_all, hp, h2p, turned, send, recv):
     net = Net(send, recv)
     peers = [net.dev(x=net.at("x", d)) for d in (1, 2, 3)]
     peers += [net.dev(y=net.at("y", d)) for d in (1, 3)]
@@ -441,30 +459,35 @@
         gather_small(net, n_all, pl.ds(0, 16), pl.ds(0, half), 0.0, 0.2),
         gather_small_turned(net, n_all, pl.ds(0, 16), pl.ds(half, half), 0.0, 0.3),
         ring(net, "x", part, lambda at: None, 0.0, 4.0),
+        products(ham, ham2, pi, hp, h2p, turned),
     ]):
         pass
     net.finish()
 
 
-def back(blk, tails):
+def back(blk, tails, ham, ham2, pi):
     lanes = blk.shape[1]
+    rows, n = ham.shape
     vm = pl.BlockSpec(memory_space=pltpu.VMEM)
     return pl.pallas_call(
         back_kernel,
         out_shape=[
             jax.ShapeDtypeStruct((blk.shape[0], 4 * lanes), BF),
             jax.ShapeDtypeStruct((NY, NZ, 2, 16, lanes), BF),
+            jax.ShapeDtypeStruct((rows, pi.shape[1]), F32),
+            jax.ShapeDtypeStruct((rows, pi.shape[1]), F32),
         ],
-        in_specs=[vm] * 2,
-        out_specs=[vm] * 2,
+        in_specs=[vm] * 5,
+        out_specs=[vm] * 4,
         scratch_shapes=[
+            pltpu.VMEM((rows, n), BF),
             pltpu.SemaphoreType.DMA((48,)),
             pltpu.SemaphoreType.DMA((48,)),
         ],
-        compiler_params=pltpu.CompilerParams(collective_id=2, has_side_effects=True, vmem_limit_bytes=8 * 1024 * 1024),
+        compiler_params=pltpu.CompilerParams(collective_id=2, has_side_effects=True, vmem_limit_bytes=22 * 1024 * 1024),
         cost_estimate=pl.CostEstimate(flops=3 * 10**10, bytes_accessed=2**20, transcendentals=0),
         name="back",
-    )(blk, tails)
+    )(blk, tails, ham, ham2, pi)
 
 
 def sums(lead, coef, aux, g_row, pall, x, pay, held):
@@ -515,20 +538,11 @@
     pay[1, :, :, 24:32, :] = jnp.broadcast_to(scal.astype(BF), (NY, NZ, 8, 2 * q))
 
 
-def modes_kernel(lead, coef, aux, ham, ham2, pi, src, u, g, hg, out, hp, h2p, turned):
+def modes_kernel(lead, coef, aux, hp, h2p, src, u, g, hg, out):
     k = pl.program_id(0)
-
-    @pl.when(k == 0)
-    def _():
-        for i in range(0, ham2.shape[0], 512):
-            turned[:, i : i + 512] = ham2[i : i + 512, :].T
-
     coupled = aux.shape[1]
-    rows = ham.shape[0]
+    rows, q = g.shape
     modes = aux.shape[0] // (2 * rows)
-    q = g.shape[1]
-    hp[...] = dot(ham[...], pi[...])
-    h2p[...] = dot(turned[...], pi[...])
     level, width, wr, wi, occ = (coef[i, k] for i in range(5))
     first = pl.multiple_of(lead[k] * coupled, coupled)
     re, im = pl.ds(first, coupled), pl.ds(pl.multiple_of(q + first, coupled), coupled)
@@ -557,11 +571,12 @@
     lax.fori_loop(0, rows // size, chunk, 0)
 
 
-def advance_modes(lead, coef, aux, ham, ham2, pi, src, u, g, hg):
-    rows, n = ham.shape
+def advance_modes(lead, coef, aux, hp, h2p, src, u, g, hg):
+    rows = hp.shape[0]
     coupled = aux.shape[1]
     modes = aux.shape[0] // (2 * rows)
     sm = pl.BlockSpec(memory_space=pltpu.SMEM)
+    block = pl.BlockSpec((rows, 2 * coupled), lambda k: (0, k))
 
     def whole(a):
         return pl.BlockSpec(a.shape, lambda k: (0,) * a.ndim)
@@ -570,14 +585,12 @@
         modes_kernel,
         grid=(modes,),
         out_shape=jax.ShapeDtypeStruct(aux.shape, F32),
-        in_specs=[sm, sm, whole(aux), whole(ham), whole(ham2), pl.BlockSpec((n, 2 * coupled), lambda k: (0, k))]
-        + [whole(a) for a in (src, u, g, hg)],
+        in_specs=[sm, sm, whole(aux), block, block] + [whole(a) for a in (src, u, g, hg)],
         out_specs=whole(aux),
-        scratch_shapes=[pltpu.VMEM((rows, 2 * coupled), F32)] * 2 + [pltpu.VMEM((rows, n), BF)],
-        compiler_params=pltpu.CompilerParams(vmem_limit_bytes=28 * 1024 * 1024),
-        cost_estimate=pl.CostEstimate(flops=4 * rows * n * 2 * coupled * modes, bytes_accessed=16 * 1024 * 1024, transcendentals=0),
+        compiler_params=pltpu.CompilerParams(vmem_limit_bytes=24 * 1024 * 1024),
+        cost_estimate=pl.CostEstimate(flops=64 * aux.size, bytes_accessed=12 * 1024 * 1024, transcendentals=0),
         name="modes",
-    )(lead, coef, aux, ham, ham2, pi, src, u, g, hg)
+    )(lead, coef, aux, hp, h2p, src, u, g, hg)
 
 
 def by_lead(x, gamma):
@@ -642,7 +655,8 @@
     own_l = lax.dynamic_slice_in_dim(l1_b, col_start - owner * rows, cols, 0)
     own_x = lax.dynamic_slice_in_dim(x_row, col_start - owner * rows, cols, 0)
     mask = (x_pos == owner).astype(BF)
-    second, n_all = back(jnp.concatenate([y.astype(BF), z.astype(BF), own_l * mask, own_x * mask], 0), tails)
+    blk = jnp.concatenate([y.astype(BF), z.astype(BF), own_l * mask, own_x * mask], 0)
+    second, n_all, h_pi, h2_pi = back(blk, tails, hamiltonian, ham2_all, pi_all)
     f_all = n_all[..., :8, :].reshape(rows, 2 * q).astype(F32)
     n_all = n_all[:, :, 0, 8:].reshape(q, 2 * q)
     third = second[2 * cols :].astype(F32)
@@ -665,9 +679,7 @@
 
     lg = jnp.concatenate([by_lead(l1_b[:, p * q : (p + 1) * q], lead_gamma) for p in range(2)], 1)
     u = 2 * H2 * (f_all + lg + dot(e_row, n_all))
-    auxiliary_rate = advance_modes(
-        lead_index, coef, aux, hamiltonian, ham2_all, pi_all, src, u, g_row, hg_row
-    ).reshape(auxiliary.shape)
+    auxiliary_rate = advance_modes(lead_index, coef, aux, h_pi, h2_pi, src, u, g_row, hg_row).reshape(auxiliary.shape)
     return density_rate, auxiliary_rate
 
 

time: 111 us -> 120 us (1.081)
  local copies, waits for them, and re-layouts: 8.28 us -> 19.1 us
  Pallas kernels: 93.3 us -> 87.3 us
  other arithmetic: 2.52 us -> 5.48 us
    unnamed x18 -> x50, local copies, waits for them, and re-layouts: 5.38 us -> 14.8 us
    pallas_call x1, Pallas kernels: 10.1 us -> 4.33 us  [advance_modes(): pl.pallas_call(modes_kernel, grid=(modes,), out_shape=jax.ShapeDtypeStruc...]
where the time goes in v5:
time: 120 us
  Pallas kernels  87.3 us (73%)
  local copies, waits for them, and re-layouts  19.1 us (16%)
  matrix products  6.85 us (6%)
  other arithmetic  5.48 us (5%)
    pallas_call x1, Pallas kernels, front(): pl.pallas_call(front_kernel, out_shape=[jax.ShapeDtypeStruct((3, cols, n)...  63 us
    pallas_call x1, Pallas kernels, back(): pl.pallas_call(back_kernel, out_shape=[jax.ShapeDtypeStruct((blk.shape[0]...  20 us
    unnamed x50, local copies, waits for them, and re-layouts  14.8 us
    dot_general x19, matrix products, dot(): lax.dot_general(a, b, (((ca,), (cb,)), ((), ())), preferred_element_type=...  6.85 us
    pallas_call x1, Pallas kernels, advance_modes(): pl.pallas_call(modes_kernel, grid=(modes,), out_shape=jax.ShapeDtypeStruc...  4.33 us

profile of v5, /device:TPU:1, one launch (start us, length us, event | category | flops | bytes accessed | tf_op | source)
XLA Modules:
  0.0 119.7 jit_solution(3659496312227349915)
XLA Ops:
  0.6 1.0 dynamic-slice_bitcast_fusion
  1.7 0.9 convert_element_type.48
  2.7 0.8 slice_bitcast_fusion.6
  3.4 0.7 stack.24.coef
  4.1 1.6 %copy-done = bf16[512,2048]{1,0:T(8,128)(2,1)S(1)} copy-done((bf16[512,2048]{1,0:T(8,128)(2,1)S(1)}, bf16[512,2048]{1,0:T(8,128)(2,1)}, u32[]{:S(2)}) %copy-start) | copy-done | bytes 2097176
  5.7 1.6 %copy-done.2 = f32[512,4,2,128]{3,2,1,0:T(2,128)S(1)} copy-done((f32[512,4,2,128]{3,2,1,0:T(2,128)S(1)}, f32[512,4,2,128]{3,2,1,0:T(2,128)}, u32[]{:S(2)}) %copy-start.2) | copy-done | bytes 2097176
  7.3 0.8 copy-done.8
  8.2 0.7 copy-done.10
  8.8 0.7 copy-done.12
  9.5 63.0 %front.1 = (bf16[3,32,2048]{2,1,0:T(8,128)(2,1)S(1)}, f32[64,512]{1,0:T(8,128)S(1)}, bf16[32,2048]{1,0:T(8,128)(2,1)S(1)}, bf16[4,512,1024]{2,1,0:T(8,128)(2,1)S...) custom-call(s32[4]{0:T(128)S(1)} %copy-done.12, ...), custom_call_target="tpu_custom_call" | custom-call | flops 99999997952 | bytes 16777216 | tf_op jit(solution)/shard_map/front/pallas_call | solution.py:384
  72.5 1.3 %copy-done.16 = bf16[1,4,8,2,32,512]{5,4,3,2,1,0:T(8,128)(2,1)} copy-done((bf16[1,4,8,2,32,512]{5,4,3,2,1,0:T(8,128)(2,1)}, bf16[1,4,8,2,32,512]{5,4,3,2,1,0:T(8,128)(2,1)S(1)}, u32[]{:S(2)}) %copy-start.16) | copy-done | bytes 2097176
  73.8 0.7 slice_bitcast_fusion.8
  74.5 0.8 convolution_bitcast_fusion
  75.4 0.7 copy-done.14
  76.1 0.7 fusion.86
  77.1 0.7 bitcast_subtract_fusion
  78.1 1.3 %fusion.12 = f32[2,512,256]{2,1,0:T(8,128)S(1)} fusion(bf16[2,2048,512]{2,1,0:T(8,128)(2,1)S(1)} %bitcast.108, bf16[2048,256]{1,0:T(8,128)(2,1)S(1)} %get-tuple-element.25), kind=kOutput, calls=%fused_computation.25 | convolution fusion | flops 1073741824 | bytes 6291456 | tf_op jit(solution)/shard_map/dot_general | solution.py:14
  79.5 0.9 copy-done.18
  80.5 1.1 fusion.11
  81.6 0.8 dynamic-slice_multiply_fusion
  82.3 0.8 dynamic-slice_multiply_fusion.1
  83.1 1.0 convolution_convert_fusion
  84.1 2.2 %copy-done.15 = bf16[4,512,1024]{2,1,0:T(8,128)(2,1)S(1)} copy-done((bf16[4,512,1024]{2,1,0:T(8,128)(2,1)S(1)}, bf16[4,512,1024]{2,1,0:T(8,128)(2,1)}, u32[]{:S(2)}) %copy-start.15) | copy-done | bytes 4194328
  86.3 1.6 %copy-done.17 = bf16[1,4,8,2,32,512]{5,4,3,2,1,0:T(8,128)(2,1)S(1)} copy-done((bf16[1,4,8,2,32,512]{5,4,3,2,1,0:T(8,128)(2,1)S(1)}, bf16[1,4,8,2,32,512]{5,4,3,2,1,0:T(8,128)(2,1)}, u32[]{:S(2)}) %copy-start.17) | copy-done | bytes 2097176
  87.9 20.0 %back.1 = (bf16[160,2048]{1,0:T(8,128)(2,1)S(1)}, bf16[4,8,2,16,512]{4,3,2,1,0:T(8,128)(2,1)S(1)}, f32[512,1024]{1,0:T(8,128)S(1)}, f32[512,1024]{1,0:T(8,128)S(1)}) custom-call(bf16[160,512]{1,0:T(8,128)(2,1)S(1)} %pad_maximum_fusion.1.blk, f32[16,512]{1,0:T(8,128)S(1)} %get-tuple-element.26.tails, bf16[512,2048]{1,0:T(8,128)(2,1)S(1)} %copy-done.1, ...), custom_call_target="tpu_custom_call" | custom-call | flops 30000001024 | bytes 1048576 | tf_op jit(solution)/shard_map/back/pallas_call | solution.py:472
  108.7 0.4 fusion.u
  109.1 0.5 copy-done.19
  109.8 1.4 %copy-done.3 = f32[512,4,2,128]{3,2,1,0:T(2,128)S(1)} copy-done((f32[512,4,2,128]{3,2,1,0:T(2,128)S(1)}, f32[512,4,2,128]{3,2,1,0:T(2,128)}, u32[]{:S(2)}) %copy-start.3) | copy-done | bytes 2097176
  111.3 4.3 %modes.1 = f32[4096,128]{1,0:T(8,128)} custom-call(s32[4]{0:T(128)S(1)} %copy-done.13, f32[5,4]{1,0:T(8,128)S(1)} %stack.24.coef, f32[4096,128]{1,0:T(8,128)S(1)} %bitcast.113, f32[512,1024]{1,0:T(8,128)S(1)} %get-tuple-element.32.hp, f32[512,1024]{1,0:T(8,128)S(1)} %get-tuple-element.33.h2p, f32[512,512]{1,0:T(8,128)S(1)} %pad_maximum_fusion.src, ...), custom_call_target="tpu_custom_call" | custom-call | flops 33554432 | bytes 12582912 | tf_op jit(solution)/shard_map/modes/pallas_call | solution.py:584
  115.7 0.8 copy-done.5
  117.3 0.8 fusion.2
  119.0 0.7 maximum_bitcast_fusion.2
  (68 shorter events, 3.8 us)
Async XLA Ops:
  4.1 1.6 %copy-start = (bf16[512,2048]{1,0:T(8,128)(2,1)S(1)}, bf16[512,2048]{1,0:T(8,128)(2,1)}, u32[]{:S(2)}) copy-start(bf16[512,2048]{1,0:T(8,128)(2,1)} %ham.3) | copy-start | bytes 6291460
  5.7 1.6 %copy-start.2 = (f32[512,4,2,128]{3,2,1,0:T(2,128)S(1)}, f32[512,4,2,128]{3,2,1,0:T(2,128)}, u32[]{:S(2)}) copy-start(f32[512,4,2,128]{3,2,1,0:T(2,128)} %param.11) | copy-start | bytes 6291460
  7.3 0.8 copy-start.8
  8.2 0.7 copy-start.10
  8.8 0.7 copy-start.12
  72.5 1.3 %copy-start.16 = (bf16[1,4,8,2,32,512]{5,4,3,2,1,0:T(8,128)(2,1)}, bf16[1,4,8,2,32,512]{5,4,3,2,1,0:T(8,128)(2,1)S(1)}, u32[]{:S(2)}) copy-start(bf16[1,4,8,2,32,512]{5,4,3,2,1,0:T(8,128)(2,1)S(1)} %get-tuple-element.27) | copy-start | bytes 6291460
  73.8 1.5 %copy-start.4 = (bf16[512,256]{1,0:T(8,128)(2,1)}, bf16[512,256]{1,0:T(8,128)(2,1)S(1)}, u32[]{:S(2)}) copy-start(bf16[512,256]{1,0:T(8,128)(2,1)S(1)} %get-tuple-element.30) | copy-start | bytes 786436
  73.8 1.6 %copy-start.6 = (f32[512,256]{1,0:T(8,128)}, f32[512,256]{1,0:T(8,128)S(1)}, u32[]{:S(2)}) copy-start(f32[512,256]{1,0:T(8,128)S(1)} %get-tuple-element.35.hg) | copy-start | bytes 1572868
  73.8 2.3 %copy-start.14 = (bf16[4,512,1024]{2,1,0:T(8,128)(2,1)}, bf16[4,512,1024]{2,1,0:T(8,128)(2,1)S(1)}, u32[]{:S(2)}) copy-start(bf16[4,512,1024]{2,1,0:T(8,128)(2,1)S(1)} %get-tuple-element.28) | copy-start | bytes 12582916
  76.7 1.3 %copy-start.20 = (bf16[512,512]{1,0:T(8,128)(2,1)}, bf16[512,512]{1,0:T(8,128)(2,1)S(1)}, u32[]{:S(2)}) copy-start(bf16[512,512]{1,0:T(8,128)(2,1)S(1)} %slice_bitcast_fusion.3) | copy-start | bytes 1572868
  79.4 1.0 copy-start.18
  80.5 3.6 %copy-start.1 = (bf16[512,2048]{1,0:T(8,128)(2,1)S(1)}, bf16[512,2048]{1,0:T(8,128)(2,1)}, u32[]{:S(2)}) copy-start(bf16[512,2048]{1,0:T(8,128)(2,1)} %ham.3) | copy-start | bytes 6291460
  84.1 2.2 %copy-start.15 = (bf16[4,512,1024]{2,1,0:T(8,128)(2,1)S(1)}, bf16[4,512,1024]{2,1,0:T(8,128)(2,1)}, u32[]{:S(2)}) copy-start(bf16[4,512,1024]{2,1,0:T(8,128)(2,1)} %copy-done.14) | copy-start | bytes 12582916
  86.3 1.6 %copy-start.17 = (bf16[1,4,8,2,32,512]{5,4,3,2,1,0:T(8,128)(2,1)S(1)}, bf16[1,4,8,2,32,512]{5,4,3,2,1,0:T(8,128)(2,1)}, u32[]{:S(2)}) copy-start(bf16[1,4,8,2,32,512]{5,4,3,2,1,0:T(8,128)(2,1)} %copy-done.16) | copy-start | bytes 6291460
  87.9 20.1 %copy-start.9 = (bf16[2,128,128]{2,1,0:T(8,128)(2,1)S(1)}, bf16[2,128,128]{2,1,0:T(8,128)(2,1)}, u32[]{:S(2)}) copy-start(bf16[2,128,128]{2,1,0:T(8,128)(2,1)} %gamma.1) | copy-start | bytes 196612
  87.9 20.1 %copy-start.21 = (bf16[512,512]{1,0:T(8,128)(2,1)S(1)}, bf16[512,512]{1,0:T(8,128)(2,1)}, u32[]{:S(2)}) copy-start(bf16[512,512]{1,0:T(8,128)(2,1)} %copy-done.20) | copy-start | bytes 1572868
  107.9 0.8 copy-start.11
  108.4 1.2 %copy-start.19 = (f32[2,512,256]{2,1,0:T(8,128)S(1)}, f32[2,512,256]{2,1,0:T(8,128)}, u32[]{:S(2)}) copy-start(f32[2,512,256]{2,1,0:T(8,128)} %copy-done.18) | copy-start | bytes 3145732
  109.6 1.6 %copy-start.3 = (f32[512,4,2,128]{3,2,1,0:T(2,128)S(1)}, f32[512,4,2,128]{3,2,1,0:T(2,128)}, u32[]{:S(2)}) copy-start(f32[512,4,2,128]{3,2,1,0:T(2,128)} %param.11) | copy-start | bytes 6291460
  109.6 1.7 %copy-start.7 = (f32[512,256]{1,0:T(8,128)S(1)}, f32[512,256]{1,0:T(8,128)}, u32[]{:S(2)}) copy-start(f32[512,256]{1,0:T(8,128)} %copy-done.6) | copy-start | bytes 1572868
  109.6 1.7 %copy-start.13 = (s32[4]{0:T(128)S(1)}, s32[4]{0:T(128)}, u32[]{:S(2)}) copy-start(s32[4]{0:T(128)} %lead.3) | copy-start | bytes 52
  115.6 0.9 copy-start.5
  115.6 1.3 %copy-start.22 = (bf16[512,512]{1,0:T(8,128)(2,1)S(1)}, bf16[512,512]{1,0:T(8,128)(2,1)}, u32[]{:S(2)}) copy-start(bf16[512,512]{1,0:T(8,128)(2,1)} %fusion.11) | copy-start | bytes 1572868
  115.6 1.7 %copy-start.24 = (f32[2,32,512]{2,1,0:T(8,128)S(1)}, f32[2,32,512]{2,1,0:T(8,128)}, u32[]{:S(2)}) copy-start(f32[2,32,512]{2,1,0:T(8,128)} %get-tuple-element.46) | copy-start | bytes 393220
  115.7 2.4 %copy-start.23 = (f32[64,512]{1,0:T(8,128)S(1)}, f32[64,512]{1,0:T(8,128)}, u32[]{:S(2)}) copy-start(f32[64,512]{1,0:T(8,128)} %get-tuple-element.44) | copy-start | bytes 393220
